TPU v7x, 32 devices: a whole 2x2x4 slice. The times are simulated.
32 devices in a mesh: tm: 4 (over y, core), space: 8 (over z, x).
Axes of the slice: x: 2, y: 2, z: 4, core: 2. Of those that a mesh axis runs over, the one named last changes fastest.
Arguments:
- perm_field: float32 [4, 32, 32, 256], P(None, 'space'), may hold values from 0.5 to 2
- step_multiplier: float32 [4, 32, 32, 256], P('tm', 'space'), may hold values from 0.5 to 2
- inflow: float32 [4, 32, 32, 256], P('tm', 'space'), may hold values from -3 to 3
- start_pressure: float32 [32, 32, 256], P('space'), may hold values from -6 to 6
- start_saturation: float32 [32, 32, 256], P('space'), may hold values from 0.1 to 0.9
- region_ids: int32 [32, 32, 256], P('space'), may hold values from 0 to 7
- region_table: float32 [3, 8], replicated, may hold values from 0.25 to 2
- well_cells: int32 [32], replicated, may hold values from 0 to 262143
- well_rates: float32 [4, 32], P('tm'), may hold values from -8 to 8
- observed: float32 [4, 4, 32], P(None, 'tm'), may hold values from -6 to 6
Outputs:
- misfit: float32 [4], replicated
- slab_pressure: float32 [4, 4, 32, 32, 256], P('tm', None, 'space')
- slab_saturation: float32 [4, 4, 32, 32, 256], P('tm', None, 'space')
All inputs are finite; a program needn't handle non-finite values.
Results may differ from a plain program's by a relative error of at most 0.0003.
Values sent between devices are 32-bit elements; how exact they have to be, the bound alone decides.
A program may use at most 64 MiB of HBM per device.

v0:
```python
import functools

import jax
import jax.numpy as jnp
from jax import lax
from jax.experimental import pallas as pl
from jax.experimental.pallas import tpu as pltpu
from jax.sharding import PartitionSpec as P

ITERS = 3
MESH = pl.DeviceIdType.MESH
EXACT = lax.Precision.HIGHEST


def before(v, axis):
    return pltpu.roll(v, 1, axis)


def after(v, axis):
    return pltpu.roll(v, v.shape[axis] - 1, axis)


def kernel(
    T, N,
    perm, mult, infl, p0, s0, ids, table, small, rows_row,
    mis, outp, outs,
    PM, IDS, M, I, SM, MH, PH, HP, HF, PB, SB, FE, TX, TZP, TZM, TYP, TYM, RC, C, V, G, B, Q, E0, E1, E2, ES,
    sM, rM, sI, rI, sS, rS, sMH, rMH, sPH, rPH, sHP, rHP, sHF, rHF, sO, rO, lO, s1, r1, s2, r2,
    fM, fI, fMH, lIN,
):
    t = lax.axis_index("tm")
    i = lax.axis_index("space")
    X, Z, Y = IDS.shape
    R = T
    loads = [
        pltpu.make_async_copy(src, dst, lIN.at[n])
        for n, (src, dst) in enumerate((
            (mult.at[0], M.at[t]), (p0, PB.at[0]), (perm.at[t], PM), (infl.at[0], I.at[t]),
            (ids, IDS), (s0, SB.at[0]),
        ))
    ]
    for load in loads:
        load.start()
    W = small.shape[0]
    K = R * ITERS
    has = (i > 0, i < N - 1)
    beside = (i - 1, i + 1)
    edge = (0, X - 1)
    order = [0, X - 1] + list(range(1, X - 1))

    def rdma(src, dst, ss, rs, dev):
        return pltpu.make_async_remote_copy(
            src_ref=src, dst_ref=dst, send_sem=ss, recv_sem=rs, device_id=dev, device_id_type=MESH
        )

    def halo(side, src, dst_slots, ss, rs, peer=None):
        return rdma(
            src, dst_slots.at[1 - side], ss.at[side], rs.at[1 - side],
            (t if peer is None else peer, beside[side]),
        )

    def send_edge(side, src, slots, ss, rs, peer=None):
        @pl.when(has[side])
        def _():
            halo(side, src, slots, ss, rs, peer).start()

    def edge_sent(side, src, slots, ss, rs, peer=None):
        @pl.when(has[side])
        def _():
            halo(side, src, slots, ss, rs, peer).wait_send()

    def edge_here(side, slots, ss, rs):
        @pl.when(has[side])
        def _():
            rdma(slots.at[side], slots.at[side], ss.at[side], rs.at[side], (t, beside[side])).wait_recv()

    def peers():
        return [(d, lax.rem(t + d, T)) for d in range(1, T)]

    barrier = pltpu.get_barrier_semaphore()

    def greet(device):
        pl.semaphore_signal(barrier, inc=1, device_id=device, device_id_type=MESH)

    for d, peer in peers():
        greet((peer, i))
    for d in range(1, N):
        greet((t, lax.rem(i + d, N)))
    for side in (0, 1):
        @pl.when(has[side])
        def _():
            for d, peer in peers():
                greet((peer, beside[side]))

    sides = jnp.where(has[0], 1, 0) + jnp.where(has[1], 1, 0)
    pl.semaphore_wait(barrier, (N - 1) + (T - 1) + (T - 1) * sides)

    mate = t + 1 - 2 * lax.rem(t, 2)

    def targets():
        return [(0, mate)] + [(d, lax.rem(t + 2 * d, T)) for d in range(1, T // 2)]

    def send_fields():
        for d, peer in targets():
            rdma(M.at[t], M.at[t], sM.at[d], rM.at[t], (peer, i)).start()
        for side in (0, 1):
            for d, peer in targets():
                send_edge(side, M.at[t, edge[side]], MH.at[t], sMH.at[d + 1], rMH.at[t], peer)
        for d, peer in targets():
            rdma(I.at[t], I.at[t], sI.at[d], rI.at[t], (peer, i)).start()

    def passes_on(r):
        return jnp.logical_and(lax.rem(t, 2) == lax.rem(r, 2), t != r)

    def pass_on(r):
        @pl.when(passes_on(r))
        def _():
            rdma(M.at[r], M.at[r], sM.at[1], rM.at[r], (r, i)).wait_recv()
            rdma(M.at[r], M.at[r], fM.at[r], rM.at[r], (mate, i)).start()
            for side in (0, 1):
                edge_here(side, MH.at[r], sMH.at[0], rMH.at[r])

                @pl.when(has[side])
                def _():
                    rdma(
                        MH.at[r, side], MH.at[r, side], fMH.at[r, side], rMH.at[r, side], (mate, i)
                    ).start()
            rdma(I.at[r], I.at[r], sI.at[1], rI.at[r], (r, i)).wait_recv()
            rdma(I.at[r], I.at[r], fI.at[r], rI.at[r], (mate, i)).start()

    for n in range(3):
        loads[n].wait()
    for side in (0, 1):
        send_edge(side, M.at[t, edge[side]], MH.at[t], sMH.at[0], rMH.at[t])
    loads[3].wait()

    @pl.when(t == 0)
    def _():
        send_fields()

    for side in (0, 1):
        send_edge(side, PM.at[edge[side]], PH, sPH, rPH)
        send_edge(side, PB.at[0, edge[side]], HP.at[0], sHP.at[0], rHP.at[0])
    for d, peer in peers():
        rdma(small, SM.at[t], sS.at[d], rS.at[t], (peer, i)).start()

    for side in (0, 1):
        @pl.when(jnp.logical_not(has[side]))
        def _():
            zero = jnp.zeros((Z, Y), jnp.float32)
            PH[side] = zero

            def clear(n, c):
                HP[n, side] = zero
                return c

            lax.fori_loop(0, K + 1, clear, 0)

            def clear_r(n, c):
                HF[n, side] = zero
                MH[n, side] = zero
                return c

            lax.fori_loop(0, R, clear_r, 0)

    SM[t] = small[...]
    loads[4].wait()
    loads[5].wait()

    def fraction(s, v):
        sq = s * s
        rest = (1.0 - s) * (1.0 - s)
        return sq / (sq + v * rest)

    for x in order:
        rock = IDS[x]
        c = jnp.zeros((Z, Y), jnp.float32)
        v = c
        g = c
        for k in range(table.shape[1]):
            hit = rock == k
            c = jnp.where(hit, table[0, k], c)
            v = jnp.where(hit, table[1, k], v)
            g = jnp.where(hit, table[2, k], g)
        C[x] = c
        V[x] = v
        G[x] = 0.1 * g
        FE[0, x] = fraction(SB[0, x], v)
    for side in (0, 1):
        send_edge(side, FE.at[0, edge[side]], HF.at[0], sHF.at[0], rHF.at[0])

    lane = lax.broadcasted_iota(jnp.int32, (W, small.shape[1]), 1)

    def column(block, n):
        return jnp.sum(jnp.where(lane == n, block, 0.0), axis=1, keepdims=True)

    base = (i * (X * Z)).astype(jnp.float32)
    local_col = column(small[...], T + 1) - base
    cols = column(small[...], T + 2)
    pick_rows = jnp.where(
        lax.broadcasted_iota(jnp.int32, (W, X * Z), 1).astype(jnp.float32) == local_col, 1.0, 0.0
    )
    pick_cols = jnp.where(
        lax.broadcasted_iota(jnp.int32, (W, Y), 1).astype(jnp.float32) == cols, 1.0, 0.0
    )
    put_rows = jnp.where(
        lax.broadcasted_iota(jnp.int32, (X * Z, W), 0).astype(jnp.float32) == rows_row[...] - base,
        1.0, 0.0,
    )
    owned = jnp.sum(pick_rows, axis=1, keepdims=True)

    def tm_here(r, buf, ss, rs):
        @pl.when(r != t)
        def _():
            rdma(buf.at[r], buf.at[r], ss.at[1], rs.at[r], (r, i)).wait_recv()

    zi = lax.broadcasted_iota(jnp.int32, (Z, Y), 0)
    yi = lax.broadcasted_iota(jnp.int32, (Z, Y), 1)

    def coef(r):
        slot = lax.rem(r, 2)
        tm_here(r, SM, sS, rS)

        @pl.when(jnp.logical_not(passes_on(r)))
        def _():
            tm_here(r, M, sM, rM)
            for side in (0, 1):
                edge_here(side, MH.at[r], sMH.at[0], rMH.at[r])

        a = [PH[0] * MH[r, 0]] + [PM[x] * M[r, x] for x in range(X)] + [PH[1] * MH[r, 1]]
        for x in range(X + 1):
            TX[slot, x] = jnp.sqrt(a[x] * a[x + 1])
        for x in range(X):
            mid = a[x + 1]
            zp = jnp.where(zi < Z - 1, jnp.sqrt(mid * after(mid, 0)), 0.0)
            yp = jnp.where(yi < Y - 1, jnp.sqrt(mid * after(mid, 1)), 0.0)
            zm = before(zp, 0)
            ym = before(yp, 1)
            TZP[slot, x] = zp
            TZM[slot, x] = zm
            TYP[slot, x] = yp
            TYM[slot, x] = ym
            RC[slot, x] = 1.0 / (C[x] + (TX[slot, x] + TX[slot, x + 1] + zp + zm + yp + ym))
        rate = column(SM[r], 0)
        Q[slot] = jnp.dot(put_rows, pick_cols * rate, precision=EXACT).reshape(X, Z, Y)

    def start_step(r):
        slot = lax.rem(r, 2)

        @pl.when(jnp.logical_not(passes_on(r)))
        def _():
            tm_here(r, I, sI, rI)

        for x in range(X):
            B[x] = C[x] * PB[r * ITERS, x] + Q[slot, x] + I[r, x]

    def sweep(r, k):
        slot = lax.rem(r, 2)
        for n, x in enumerate(order):
            if x == 0:
                edge_here(0, HP.at[k], sHP.at[k], rHP.at[k])
                left = HP[k, 0]
            else:
                left = PB[k, x - 1]
            if x == X - 1:
                edge_here(1, HP.at[k], sHP.at[k], rHP.at[k])
                right = HP[k, 1]
            else:
                right = PB[k, x + 1]
            p = PB[k, x]
            total = B[x] + TX[slot, x] * left + TX[slot, x + 1] * right
            total = total + TZP[slot, x] * after(p, 0) + TZM[slot, x] * before(p, 0)
            total = total + TYP[slot, x] * after(p, 1) + TYM[slot, x] * before(p, 1)
            PB[k + 1, x] = total * RC[slot, x]
            if n < 2:
                send_edge(n, PB.at[k + 1, x], HP.at[k + 1], sHP.at[k + 1], rHP.at[k + 1])

    parts = ((0, 0, X), (1, 1, X - 2), (2, 0, 1), (3, X - 1, 1))

    def piece(which, r, member):
        _, at, many = parts[which]
        rows = pl.ds(at, many)
        if which == 0:
            return PB.at[(r + 1) * ITERS, rows], outp.at[0, member, rows]
        return SB.at[r + 1, rows], outs.at[0, member, rows]

    def put_out(r, which):
        src, dst = piece(which, r, t)

        @pl.when(r != t)
        def _():
            rdma(src, dst, sO.at[r, which], rO.at[t, which], (r, i)).start()

        @pl.when(r == t)
        def _():
            pltpu.make_async_copy(src, dst, lO.at[which]).start()

    def transport(r, last=False):
        slot = lax.rem(r, 2)
        k = (r + 1) * ITERS
        def face(coupling, pi, pj, fi, fj):
            flux = coupling * (pi - pj)
            return flux * jnp.where(flux > 0, fi, fj)

        def p_of(x):
            return HP[k, 0] if x < 0 else (HP[k, 1] if x >= X else PB[k, x])

        def f_of(x):
            return HF[r, 0] if x < 0 else (HF[r, 1] if x >= X else FE[r, x])

        for x in order[2:] + order[:2]:
            if x in edge:
                side = edge.index(x)
                if side == 0:
                    put_out(r, 1)
                edge_here(side, HF.at[r], sHF.at[r], rHF.at[r])
                if last:
                    edge_here(side, HP.at[k], sHP.at[k], rHP.at[k])
            p = p_of(x)
            f = f_of(x)
            s = SB[r, x]
            q = Q[slot, x]
            out = face(TX[slot, x + 1], p, p_of(x + 1), f, f_of(x + 1))
            out = out - face(TX[slot, x], p_of(x - 1), p, f_of(x - 1), f)
            cz = face(TZP[slot, x], p, after(p, 0), f, after(f, 0))
            cy = face(TYP[slot, x], p, after(p, 1), f, after(f, 1))
            out = out + (cz - before(cz, 0)) + (cy - before(cy, 1))
            gained = jnp.maximum(q, 0.0) * (1.0 - s) - jnp.maximum(-q, 0.0) * f - out
            s = s + G[x] * gained
            SB[r + 1, x] = s
            if not last:
                FE[r + 1, x] = fraction(s, V[x])
            if x in edge:
                put_out(r, 2 + edge.index(x))

        @pl.when(r < R - 1)
        def _():
            for side in (0, 1):
                send_edge(side, FE.at[r + 1, edge[side]], HF.at[r + 1], sHF.at[r + 1], rHF.at[r + 1])

    pass_on(0)

    @pl.when(t > 0)
    def _():
        send_fields()

    for side in (0, 1):
        edge_here(side, PH, sPH, rPH)
    coef(0)
    ES[...] = jnp.zeros(ES.shape, jnp.float32)

    def step(r, carry):
        k = r * ITERS
        start_step(r)
        sweep(r, k)

        @pl.when(r > 0)
        def _():
            transport(r - 1)

        @pl.when(r < R - 1)
        def _():
            pass_on(r + 1)

        for j in range(1, ITERS):
            sweep(r, k + j)
            if j == 1:
                @pl.when(r < R - 1)
                def _():
                    coef(r + 1)
        put_out(r, 0)
        seen = jnp.dot(pick_rows, PB[k + ITERS].reshape(X * Z, Y), precision=EXACT)
        predicted = jnp.sum(seen * pick_cols, axis=1, keepdims=True)
        gap = predicted - column(SM[r], 1 + t)
        ES[...] = ES[...] + owned * gap * gap
        return carry

    lax.fori_loop(0, R, step, 0)

    E0[...] = jnp.broadcast_to(jnp.sum(ES[...], axis=0, keepdims=True), E0.shape)
    others = [(d, lax.rem(i + d, N)) for d in range(1, N)]
    for d, peer in others:
        rdma(E0, E1.at[i], s1.at[d], r1.at[i], (t, peer)).start()
    transport(R - 1, True)
    E1[i] = E0[...]
    for d, peer in others:
        rdma(E1.at[peer], E1.at[peer], s1.at[d], r1.at[peer], (t, peer)).wait_recv()
    whole = E1[0]
    for n in range(1, N):
        whole = whole + E1[n]
    mine = lax.broadcasted_iota(jnp.int32, whole.shape, 1) == t
    E2[t] = jnp.where(mine, whole, 0.0)
    for d, peer in peers():
        rdma(E2.at[t], E2.at[t], s2.at[d], r2.at[t], (peer, i)).start()
    for d, peer in peers():
        rdma(E2.at[peer], E2.at[peer], s2.at[d], r2.at[peer], (peer, i)).wait_recv()
    result = E2[0]
    for n in range(1, T):
        result = result + E2[n]
    mis[...] = result * (1.0 / (R * W))

    for side in (0, 1):
        edge_sent(side, M.at[t, edge[side]], MH.at[t], sMH.at[0], rMH.at[t])
        edge_sent(side, PM.at[edge[side]], PH, sPH, rPH)

        def sent_k(k, c):
            edge_sent(side, PB.at[k, edge[side]], HP.at[k], sHP.at[k], rHP.at[k])
            return c

        lax.fori_loop(0, K + 1, sent_k, 0)

        def sent_r(r, c):
            edge_sent(side, FE.at[r, edge[side]], HF.at[r], sHF.at[r], rHF.at[r])

            @pl.when(jnp.logical_and(passes_on(r), has[side]))
            def _():
                rdma(
                    MH.at[r, side], MH.at[r, side], fMH.at[r, side], rMH.at[r, side], (mate, i)
                ).wait_send()
            return c

        lax.fori_loop(0, R, sent_r, 0)
        for d, peer in targets():
            edge_sent(side, M.at[t, edge[side]], MH.at[t], sMH.at[d + 1], rMH.at[t], peer)

    def sent_on(r, c):
        @pl.when(passes_on(r))
        def _():
            rdma(M.at[r], M.at[r], fM.at[r], rM.at[r], (mate, i)).wait_send()
            rdma(I.at[r], I.at[r], fI.at[r], rI.at[r], (mate, i)).wait_send()
        return c

    lax.fori_loop(0, R, sent_on, 0)
    for d, peer in targets():
        rdma(M.at[t], M.at[t], sM.at[d], rM.at[t], (peer, i)).wait_send()
        rdma(I.at[t], I.at[t], sI.at[d], rI.at[t], (peer, i)).wait_send()
    for d, peer in peers():
        rdma(small, SM.at[t], sS.at[d], rS.at[t], (peer, i)).wait_send()
        rdma(E2.at[t], E2.at[t], s2.at[d], r2.at[t], (peer, i)).wait_send()
    for d, peer in others:
        rdma(E0, E1.at[i], s1.at[d], r1.at[i], (t, peer)).wait_send()
    for which in range(len(parts)):
        for d, peer in peers():
            src, dst = piece(which, peer, t)
            rdma(src, dst, sO.at[peer, which], rO.at[t, which], (peer, i)).wait_send()
            src, dst = piece(which, t, peer)
            rdma(src, dst, sO.at[peer, which], rO.at[peer, which], (peer, i)).wait_recv()
        src, dst = piece(which, t, t)
        pltpu.make_async_copy(src, dst, lO.at[which]).wait()


def body(
    perm_field, step_multiplier, inflow, start_pressure, start_saturation,
    region_ids, region_table, well_cells, well_rates, observed,
):
    T = lax.axis_size("tm")
    N = lax.axis_size("space")
    X, Z, Y = start_pressure.shape
    W = well_cells.shape[0]
    members = perm_field.shape[0]
    assert members == T and T % 2 == 0 and step_multiplier.shape[0] == 1
    well_row = (well_cells // Y).astype(jnp.float32)
    well_col = (well_cells % Y).astype(jnp.float32)
    small = jnp.concatenate(
        [well_rates, observed[:, 0, :], well_row[None], well_col[None]], axis=0
    ).T
    small = jnp.pad(small, ((0, 0), (0, 128 - small.shape[1])))
    K = T * ITERS
    f32 = jnp.float32
    cell = (Z, Y)
    block = (X, Z, Y)

    def buf(*shape):
        return pltpu.VMEM(shape, f32)

    dma = pltpu.SemaphoreType.DMA
    vmem = pl.BlockSpec(memory_space=pltpu.VMEM)
    anyspace = pl.BlockSpec(memory_space=pl.ANY)
    out_shape = jax.ShapeDtypeStruct((1, members) + block, f32)
    mis, outp, outs = pl.pallas_call(
        functools.partial(kernel, T, N),
        out_shape=(jax.ShapeDtypeStruct((8, 128), f32), out_shape, out_shape),
        in_specs=[anyspace] * 6 + [pl.BlockSpec(memory_space=pltpu.SMEM)] + [vmem] * 2,
        out_specs=(vmem, anyspace, anyspace),
        scratch_shapes=[
            buf(*block), pltpu.VMEM(block, jnp.int32),
            buf(T, *block), buf(T, *block), buf(T, W, 128), buf(T, 2, *cell), buf(2, *cell),
            buf(K + 1, 2, *cell), buf(T, 2, *cell), buf(K + 1, *block), buf(T + 1, *block),
            buf(T + 1, *block), buf(2, X + 1, *cell), buf(2, *block), buf(2, *block),
            buf(2, *block), buf(2, *block), buf(2, *block), buf(*block), buf(*block), buf(*block),
            buf(*block), buf(2, *block), buf(8, 128), buf(N, 8, 128), buf(T, 8, 128), buf(W, 1),
            dma((T,)), dma((T,)), dma((T,)), dma((T,)), dma((T,)), dma((T,)),
            dma((T, 2)), dma((T, 2)), dma((2,)), dma((2,)), dma((K + 1, 2)), dma((K + 1, 2)),
            dma((T, 2)), dma((T, 2)), dma((T, 4)), dma((T, 4)), dma((4,)),
            dma((N,)), dma((N,)), dma((T,)), dma((T,)),
            dma((T,)), dma((T,)), dma((T, 2)), dma((6,)),
        ],
        compiler_params=pltpu.CompilerParams(
            has_side_effects=True, collective_id=0
        ),
    )(
        perm_field, step_multiplier, inflow, start_pressure, start_saturation, region_ids,
        region_table, small, well_row[None],
    )
    return mis[0, :members], outp, outs


def solution(mesh):
    return jax.shard_map(
        body,
        mesh=mesh,
        in_specs=(
            P(None, "space", None, None),
            P("tm", "space", None, None),
            P("tm", "space", None, None),
            P("space", None, None),
            P("space", None, None),
            P("space", None, None),
            P(),
            P(),
            P("tm", None),
            P(None, "tm", None),
        ),
        out_specs=(P(), P("tm", None, "space", None, None), P("tm", None, "space", None, None)),
        check_vma=False,
    )
```

profile of v0, /device:TPU:0, one launch (start us, length us, event | category | flops | bytes accessed | tf_op | source)
XLA Modules:
  0.0 72.3 jit_solution(4763355131174911716)
XLA Ops:
  0.6 0.0 copy-start.4
  0.6 0.6 copy-done.4
  1.3 0.0 copy-start.1
  1.3 0.0 copy-start.2
  1.3 0.0 copy-start.3
  1.3 0.5 copy-done.1
  1.8 0.2 copy-done.2
  2.0 0.0 copy-done.3
  2.0 0.1 copy.17
  2.1 0.6 pad.4.small
  2.7 65.6 %shard_map.121 = (f32[8,128]{1,0:T(8,128)}, f32[1,4,4,32,256]{4,3,2,1,0:T(8,128)}, f32[1,4,4,32,256]{4,3,2,1,0:T(8,128)}) custom-call(f32[4,4,32,256]{3,2,1,0:T(8,128)} %perm.1, f32[1,4,32,256]{3,2,1,0:T(8,128)} %mult.1, f32[1,4,32,256]{3,2,1,0:T(8,128)} %infl.1, f32[4,32,256]{2,1,0:T(8,128)} %p0.1, f32[4,32,256]{2,1,0:T(8,128)} %s0.1, s32[4,32,256]{2,1,0:T(8,128)} %ids.1, ...), custom_call_target="tpu_custom_call" | custom-call | tf_op jit(solution)/shard_map/pallas_call | solution.py:480
  68.4 1.2 %slice_bitcast_fusion = f32[4]{0:T(128)} fusion(f32[8,128]{1,0:T(8,128)} %get-tuple-element.6), kind=kLoop, calls=%fused_computation.8 | loop fusion | bytes 32 | tf_op jit(solution)/shard_map/squeeze | solution.py:505
  69.6 0.0 copy-start
  69.6 1.9 %copy.20 = f32[1,4,4,32,256]{4,3,2,1,0:T(8,128)} copy(f32[1,4,4,32,256]{4,3,2,1,0:T(8,128)} %get-tuple-element.15) | data formatting | bytes 1048576
  71.5 0.0 copy-done
  71.5 0.8 %copy.21 = f32[1,4,4,32,256]{4,3,2,1,0:T(8,128)} copy(f32[1,4,4,32,256]{4,3,2,1,0:T(8,128)S(1)} %copy-done) | data formatting | bytes 1048576
  (2 shorter events, 0.0 us)
Async XLA Ops:
  0.6 0.7 copy-start.4
  1.3 0.5 copy-start.1
  1.3 0.7 copy-start.2
  1.3 0.7 copy-start.3
  69.6 1.9 %copy-start = (f32[1,4,4,32,256]{4,3,2,1,0:T(8,128)S(1)}, f32[1,4,4,32,256]{4,3,2,1,0:T(8,128)}, u32[]{:S(2)}) copy-start(f32[1,4,4,32,256]{4,3,2,1,0:T(8,128)} %get-tuple-element.16) | copy-start | bytes 1572868
where the time goes:
time: 72.5 us; the launch traced here: 72.3 us
  Pallas kernels  65.6 us (90%)
  local copies, waits for them, and re-layouts  5.95 us (8%)
    pallas_call x1, Pallas kernels, body(): pl.pallas_call(functools.partial(kernel, T, N), out_shape=(jax.ShapeDtype...  65.6 us
    unnamed x12, local copies, waits for them, and re-layouts  4.06 us

commit v1 on v0

v1 whole, which is shorter than its diff:
```python
import functools

import jax
import jax.numpy as jnp
from jax import lax
from jax.experimental import pallas as pl
from jax.experimental.pallas import tpu as pltpu
from jax.sharding import PartitionSpec as P

ITERS = 3
H = ITERS + 1
MESH = pl.DeviceIdType.MESH
EXACT = lax.Precision.HIGHEST


def before(v, axis):
    return pltpu.roll(v, 1, axis)


def after(v, axis):
    return pltpu.roll(v, v.shape[axis] - 1, axis)


def kernel(
    T, N,
    perm, mult, infl, p0, s0, ids, table, small, rows_row,
    mis, outp, outs,
    PM, IDS, MS, IW, CW, SA, SO, PB, PX, SM, RC, SS, EE, QI, BB, DD, WW,
    IDW, SB, FE, HF, V, G, Q, ES, E0, E1, E2,
    lIN, sF, rF, sS, rS, sX, rX, sP, rP, sM, rM, sA, rA, sHF, rHF, sO, rO, lO, s1, r1, s2, r2,
):
    t = lax.axis_index("tm")
    i = lax.axis_index("space")
    X, Z, Y = IDS.shape
    R = T
    W = small.shape[0]
    U = N // 2
    XU = 2 * X
    WL = XU + 2 * H
    row = t // 2
    core = lax.rem(t, 2)
    u = i // 2
    h = lax.rem(i, 2)
    mate = t + 1 - 2 * core
    pair = i + 1 - 2 * h
    member = 2 * row + h
    own = H + h * X
    toward = 2 * h - 1
    side_here = (u > 0, u < U - 1)
    edge_there = jnp.logical_or(jnp.logical_and(h == 1, u < U - 1), jnp.logical_and(h == 0, u > 0))

    def load(n, src, dst):
        return pltpu.make_async_copy(src, dst, lIN.at[n])

    def rdma(src, dst, ss, rs, dev):
        return pltpu.make_async_remote_copy(
            src_ref=src, dst_ref=dst, send_sem=ss, recv_sem=rs, device_id=dev, device_id_type=MESH
        )

    mult_in = load(0, mult.at[0], MS.at[t])
    infl_in = load(1, infl.at[0], IW.at[t, pl.ds(own, X)])
    ids_in = load(2, ids, IDS)
    perm_in = load(3, perm.at[pl.ds(2 * row, 2)], PM)
    p0_in = load(4, p0, PB.at[0, pl.ds(own, X)])
    s0_in = load(3, s0, SB.at[0, pl.ds(h * X, X)])
    ids_win = load(4, ids, IDW.at[pl.ds(h * X, X)])
    mult_in.start()
    infl_in.start()

    @pl.when(core == 1)
    def _():
        perm_in.start()
        p0_in.start()
        ids_in.start()

    @pl.when(core == 0)
    def _():
        s0_in.start()
        ids_win.start()

    barrier = pltpu.get_barrier_semaphore()

    def greet(device):
        pl.semaphore_signal(barrier, inc=1, device_id=device, device_id_type=MESH)

    for d in range(1, T):
        peer = lax.rem(t + d, T)
        greet((peer, i))
        greet((peer, pair))
    for d in range(1, N):
        greet((t, lax.rem(i + d, N)))

    zi = lax.broadcasted_iota(jnp.int32, (Z, Y), 0)
    yi = lax.broadcasted_iota(jnp.int32, (Z, Y), 1)
    zero = jnp.zeros((Z, Y), jnp.float32)

    def neighbours(at, x):
        w = at(x)
        total = at(x - 1) + at(x + 1)
        total = total + (
            jnp.where(zi < Z - 1, after(w, 0), 0.0) + jnp.where(zi > 0, before(w, 0), 0.0)
        )
        return total + (
            jnp.where(yi < Y - 1, after(w, 1), 0.0) + jnp.where(yi > 0, before(w, 1), 0.0)
        )

    def looked_up(rock, which):
        v = zero
        for k in range(table.shape[1]):
            v = jnp.where(rock == k, table[which, k], v)
        return v

    lane = lax.broadcasted_iota(jnp.int32, (W, small.shape[1]), 1)

    def column(block, n):
        return jnp.sum(jnp.where(lane == n, block, 0.0), axis=1, keepdims=True)

    pick_cols = jnp.where(
        lax.broadcasted_iota(jnp.int32, (W, Y), 1).astype(jnp.float32) == column(small[...], T + 2),
        1.0, 0.0,
    )

    def put_rows(first, count):
        base = (first * Z).astype(jnp.float32)
        return jnp.where(
            lax.broadcasted_iota(jnp.int32, (count * Z, W), 0).astype(jnp.float32) == rows_row[...] - base,
            1.0, 0.0,
        )

    others_t = [(d, lax.rem(t + d, T)) for d in range(1, T)]

    def small_to(d, peer):
        return rdma(small, SM.at[t], sM.at[d], rM.at[t], (peer, i))

    def small_here(r):
        @pl.when(r != t)
        def _():
            rdma(SM.at[r], SM.at[r], sM.at[1], rM.at[r], (r, i)).wait_recv()

    def source(r, rows, count):
        rate = column(SM[r], 0)
        return jnp.dot(rows, pick_cols * rate, precision=EXACT).reshape(count, Z, Y)

    def field_to(rr):
        dev = (2 * rr + 1, i)
        return (
            rdma(MS.at[t], MS.at[t], sF.at[0, rr], rF.at[0, t], dev),
            rdma(
                IW.at[t, pl.ds(own, X)], IW.at[t, pl.ds(own, X)], sF.at[1, rr], rF.at[1, t], dev
            ),
        )

    def each_field(act):
        for rr in range(T // 2):
            @pl.when(t != 2 * rr + 1)
            def _():
                for copy in field_to(rr):
                    act(copy)

    def send_fields():
        each_field(lambda copy: copy.start())

    def put_out(r, half, src, which):
        dst = (outp, outs)[which].at[0, member]
        here = jnp.logical_and(r == t, half == h)

        @pl.when(jnp.logical_not(here))
        def _():
            rdma(src, dst, sO.at[r, half], rO.at[which, member], (r, 2 * u + half)).start()

        @pl.when(here)
        def _():
            pltpu.make_async_copy(src, dst, lO).start()

    def outs_sent(src, which):
        def sent(r, c):
            for half in (0, 1):
                dst = (outp, outs)[which].at[0, member]
                here = jnp.logical_and(r == t, half == h)

                @pl.when(jnp.logical_not(here))
                def _():
                    rdma(src, dst, sO.at[r, half], rO.at[which, member], (r, 2 * u + half)).wait_send()
            return c

        lax.fori_loop(0, R, sent, 0)
        pltpu.make_async_copy(src, (outp, outs)[which].at[0, member], lO).wait()

    def outs_here():
        for which in (0, 1):
            for m in range(T):
                mine = jnp.logical_and(core == 1 - which, m == member)

                @pl.when(jnp.logical_not(mine))
                def _():
                    dst = (outp, outs)[which].at[0, m]
                    rdma(dst, dst, sO.at[0, 0], rO.at[which, m], (t, pair)).wait_recv()

    def misfit_here(skip):
        for m in range(T):
            wait = rdma(E2.at[m], E2.at[m], s2.at[0], r2.at[m], (t, pair))
            if skip:
                @pl.when(m != member)
                def _():
                    wait.wait_recv()
            else:
                wait.wait_recv()
        lanes = lax.broadcasted_iota(jnp.int32, (8, 128), 1)
        result = jnp.zeros((8, 128), jnp.float32)
        for m in range(T):
            result = result + jnp.where(lanes == m, E2[m], 0.0)
        mis[...] = result * (1.0 / (R * W))

    def spread(n, window, depth, same, other):
        partner = rdma(
            other.at[pl.ds(0, X)], window.at[pl.ds(own, X)], sS.at[n, 0], rS.at[n, 0], (t, pair)
        )
        start = h * (X - depth)
        there = pl.ds((1 - h) * (H + XU) + h * (H - depth), depth)
        straight = rdma(
            same.at[pl.ds(start, depth)], window.at[there], sS.at[n, 1], rS.at[n, 2 - h],
            (t, i + 2 * toward),
        )
        aslant = rdma(
            other.at[pl.ds(start, depth)], window.at[there], sS.at[n, 2], rS.at[n, 2 - h],
            (t, i + toward),
        )
        return partner, straight, aslant

    def spread_start(*args):
        partner, straight, aslant = spread(*args)
        partner.start()

        @pl.when(edge_there)
        def _():
            straight.start()
            aslant.start()

    def spread_sent(*args):
        partner, straight, aslant = spread(*args)
        partner.wait_send()

        @pl.when(edge_there)
        def _():
            straight.wait_send()
            aslant.wait_send()

    def spread_here(n, window, depth):
        part = window.at[pl.ds(H + (1 - h) * X, X)]
        rdma(part, part, sS.at[n, 0], rS.at[n, 0], (t, pair)).wait_recv()
        for side in (0, 1):
            @pl.when(side_here[side])
            def _():
                part = window.at[pl.ds(H + XU if side else H - depth, depth)]
                rdma(part, part, sS.at[n, 1], rS.at[n, 1 + side], (t, pair)).wait_recv()

    def own_of(window):
        return window.at[pl.ds(own, X)]

    def conduct_args(r):
        return r, SA.at[r], H, own_of(SA.at[r]), SO.at[r]

    def inflow_args(r):
        mine = own_of(IW.at[r])
        return R + r, IW.at[r], H - 1, mine, mine

    def pressure_args():
        mine = own_of(PB.at[0])
        return 2 * R, PB.at[0], H, mine, mine

    def storage_args():
        mine = own_of(CW)
        return 2 * R + 1, CW, H - 1, mine, mine

    def distribute(r):
        @pl.when(r != t)
        def _():
            rdma(MS.at[r], MS.at[r], sF.at[0, 0], rF.at[0, r], (r, i)).wait_recv()

        for x in range(X):
            SO[r, x] = jnp.sqrt(PM[1 - h, x] * MS[r, x])
            SA[r, own + x] = jnp.sqrt(PM[h, x] * MS[r, x])
        spread_start(*conduct_args(r))

        @pl.when(r != t)
        def _():
            mine = own_of(IW.at[r])
            rdma(mine, mine, sF.at[1, 0], rF.at[1, r], (r, i)).wait_recv()
        spread_start(*inflow_args(r))

    def round_of(k, side):
        if side == 0:
            src, dst, dev = pl.ds(H, H), pl.ds(H + XU, H), (t, i - 2)
        else:
            src, dst, dev = pl.ds(XU, H), pl.ds(0, H), (t, i + 2)
        return rdma(PB.at[k, src], PB.at[k, dst], sP.at[k, side], rP.at[k, 1 - side], dev)

    def handed(r):
        mid = pl.ds(H, XU)
        wide = pl.ds(H - 1, XU + 2)
        dev = (mate, i)
        return (
            rdma(SA.at[r, wide], SA.at[r, wide], sX.at[r, 0], rX.at[r, 0], dev),
            rdma(PB.at[r + 1, mid], PB.at[r + 1, mid], sX.at[r, 1], rX.at[r, 1], dev),
            rdma(PX.at[r], PX.at[r], sX.at[r, 2], rX.at[r, 2], dev),
        )

    def meet():
        pl.semaphore_wait(barrier, (N - 1) + 2 * (T - 1))

    @pl.when(core == 1)
    def _():
        ids_in.wait()
        for x in range(X):
            CW[own + x] = looked_up(IDS[x], 0)
        for side in (0, 1):
            @pl.when(jnp.logical_not(side_here[side]))
            def _():
                first = H + XU if side else 0
                for x in range(first, first + H):
                    CW[x] = zero + 1.0

                def clear(r, c):
                    for x in range(first, first + H):
                        SA[r, x] = zero
                        IW[r, x] = zero
                        PB[r, x] = zero
                    return c

                lax.fori_loop(0, R, clear, 0)
        p0_in.wait()
        mult_in.wait()
        infl_in.wait()
        perm_in.wait()
        meet()
        spread_start(*pressure_args())
        spread_start(*storage_args())
        for d, peer in others_t:
            small_to(d, peer).start()
        SM[t] = small[...]
        distribute(0)
        send_fields()
        rows = put_rows(u * XU - H, WL)

        def coefficients(r):
            slot = lax.rem(r, 2)
            spread_here(r, SA.at[r], H)
            handed(r)[0].start()
            for x in range(1, WL - 1):
                a = SA[r, x]
                rc = 1.0 / (CW[x] + a * neighbours(lambda y: SA[r, y], x))
                RC[slot, x] = rc
                ss = a * rc
                SS[slot, x] = ss
                EE[slot, x] = a * ss
            small_here(r)
            q = source(r, rows, WL)
            spread_here(R + r, IW.at[r], H - 1)
            for x in range(1, WL - 1):
                QI[slot, x] = q[x] + IW[r, x]

        spread_here(2 * R, PB.at[0], H)
        spread_here(2 * R + 1, CW, H - 1)
        coefficients(0)
        distribute(1)

        def step(r, carry):
            slot = lax.rem(r, 2)

            def first(layers):
                for x in layers:
                    WW[0, x] = SA[r, x] * PB[r, x]

            def sweep_one(layers):
                for x in layers:
                    b = CW[x] * PB[r, x] + QI[slot, x]
                    d = SS[slot, x] * b
                    BB[x] = b
                    DD[x] = d
                    WW[1, x] = d + EE[slot, x] * neighbours(lambda y: WW[0, y], x)

            first(range(H, H + XU))
            sweep_one(range(H + 1, H + XU - 1))

            @pl.when(r > 0)
            def _():
                for side in (0, 1):
                    @pl.when(side_here[side])
                    def _():
                        part = PB.at[r, pl.ds(H + XU if side else 0, H)]
                        rdma(part, part, sP.at[r, side], rP.at[r, side], (t, pair)).wait_recv()

            first(range(0, H))
            sweep_one(range(1, H + 1))
            first(range(H + XU, WL))
            sweep_one(range(H + XU - 1, WL - 1))
            for j in range(1, ITERS - 1):
                for x in range(j + 1, WL - j - 1):
                    WW[j + 1, x] = DD[x] + EE[slot, x] * neighbours(lambda y: WW[j, y], x)

            def last(x):
                return RC[slot, x] * (
                    BB[x] + SA[r, x] * neighbours(lambda y: WW[ITERS - 1, y], x)
                )

            def send(side):
                @pl.when(jnp.logical_and(r < R - 1, side_here[side]))
                def _():
                    round_of(r + 1, side).start()

            for x in range(H, H + X):
                PB[r + 1, x] = last(x)
            send(0)
            for x in range(H + X, H + XU):
                PB[r + 1, x] = last(x)
            send(1)
            handed(r)[1].start()
            for half in (0, 1):
                put_out(r, half, PB.at[r + 1, pl.ds(H + half * X, X)], 0)
            PX[r, 0] = last(H - 1)
            PX[r, 1] = last(H + XU)
            handed(r)[2].start()

            @pl.when(r < R - 1)
            def _():
                coefficients(r + 1)

            @pl.when(r < R - 2)
            def _():
                distribute(r + 2)
            return carry

        lax.fori_loop(0, R, step, 0)
        misfit_here(False)
        outs_here()
        outs_sent(PB.at[0, pl.ds(0, X)], 0)

        def done(r, c):
            spread_sent(*conduct_args(r))
            spread_sent(*inflow_args(r))
            for copy in handed(r):
                copy.wait_send()

            @pl.when(r > 0)
            def _():
                for side in (0, 1):
                    @pl.when(side_here[side])
                    def _():
                        round_of(r, side).wait_send()
            return c

        lax.fori_loop(0, R, done, 0)
        spread_sent(*pressure_args())
        spread_sent(*storage_args())

    @pl.when(core == 0)
    def _():
        def fraction(s, v):
            sq = s * s
            rest = (1.0 - s) * (1.0 - s)
            return sq / (sq + v * rest)

        def edge_flow(r, side):
            src = FE.at[r, XU - 1 if side else 0]
            return rdma(
                src, HF.at[r, 1 - side], sHF.at[r, side], rHF.at[r, 1 - side], (t, i + 4 * side - 2)
            )

        def send_flow(r):
            for side in (0, 1):
                @pl.when(side_here[side])
                def _():
                    edge_flow(r, side).start()

        def pair_copies():
            part = pl.ds(h * X, X)
            return (
                rdma(SB.at[0, part], SB.at[0, part], sA.at[0], rA.at[0], (t, pair)),
                rdma(IDW.at[part], IDW.at[part], sA.at[1], rA.at[1], (t, pair)),
            )

        for side in (0, 1):
            @pl.when(jnp.logical_not(side_here[side]))
            def _():
                def clear(r, c):
                    HF[r, side] = zero
                    return c

                lax.fori_loop(0, R, clear, 0)

        mult_in.wait()
        infl_in.wait()
        s0_in.wait()
        ids_win.wait()
        meet()
        send_fields()
        for d, peer in others_t:
            small_to(d, peer).start()
        SM[t] = small[...]
        for copy in pair_copies():
            copy.start()
        rows = put_rows(u * XU, XU)
        local = column(small[...], T + 1) - (u * (XU * Z)).astype(jnp.float32)
        pick_rows = jnp.where(
            lax.broadcasted_iota(jnp.int32, (W, XU * Z), 1).astype(jnp.float32) == local, 1.0, 0.0
        )
        owned = jnp.sum(pick_rows, axis=1, keepdims=True)
        there = pl.ds((1 - h) * X, X)
        rdma(SB.at[0, there], SB.at[0, there], sA.at[0], rA.at[0], (t, pair)).wait_recv()
        rdma(IDW.at[there], IDW.at[there], sA.at[1], rA.at[1], (t, pair)).wait_recv()
        for x in range(XU):
            rock = IDW[x]
            V[x] = looked_up(rock, 1)
            G[x] = 0.1 * looked_up(rock, 2)
            FE[0, x] = fraction(SB[0, x], V[x])
        send_flow(0)
        ES[...] = jnp.zeros(ES.shape, jnp.float32)

        def step(r, carry):
            small_here(r)
            q_all = source(r, rows, XU)
            for x in range(XU):
                Q[x] = q_all[x]
            for copy in handed(r):
                copy.wait_recv()
            seen = jnp.dot(pick_rows, PB[r + 1, H:H + XU].reshape(XU * Z, Y), precision=EXACT)
            predicted = jnp.sum(seen * pick_cols, axis=1, keepdims=True)
            gap = predicted - column(SM[r], 1 + member)
            ES[...] = ES[...] + owned * gap * gap

            @pl.when(r == R - 1)
            def _():
                E0[...] = jnp.broadcast_to(jnp.sum(ES[...], axis=0, keepdims=True), E0.shape)
                for d in range(1, U):
                    peer = lax.rem(u + d, U)
                    rdma(E0, E1.at[u], s1.at[d], r1.at[u], (t, 2 * peer + h)).start()

            for side in (0, 1):
                @pl.when(side_here[side])
                def _():
                    part = HF.at[r, side]
                    rdma(part, part, sHF.at[r, side], rHF.at[r, side], (t, pair)).wait_recv()

            def p_of(x):
                return PX[r, 0] if x < 0 else (PX[r, 1] if x >= XU else PB[r + 1, H + x])

            def f_of(x):
                return HF[r, 0] if x < 0 else (HF[r, 1] if x >= XU else FE[r, x])

            def face(ai, aj, pi, pj, fi, fj):
                fall = pi - pj
                return ai * aj * fall * jnp.where(fall > 0, fi, fj)

            def across(x):
                return face(SA[r, H + x - 1], SA[r, H + x], p_of(x - 1), p_of(x), f_of(x - 1), f_of(x))

            low = across(0)
            for x in range(XU):
                high = across(x + 1)
                a = SA[r, H + x]
                p = p_of(x)
                f = f_of(x)
                s = SB[r, x]
                q = Q[x]
                cz = jnp.where(zi < Z - 1, face(a, after(a, 0), p, after(p, 0), f, after(f, 0)), 0.0)
                cy = jnp.where(yi < Y - 1, face(a, after(a, 1), p, after(p, 1), f, after(f, 1)), 0.0)
                out = (high - low) + (cz - before(cz, 0)) + (cy - before(cy, 1))
                low = high
                gained = jnp.maximum(q, 0.0) * (1.0 - s) - jnp.maximum(-q, 0.0) * f - out
                s = s + G[x] * gained
                SB[r + 1, x] = s
                FE[r + 1, x] = fraction(s, V[x])
                if x == X - 1:
                    put_out(r, 0, SB.at[r + 1, pl.ds(0, X)], 1)
            put_out(r, 1, SB.at[r + 1, pl.ds(X, X)], 1)

            @pl.when(r < R - 1)
            def _():
                send_flow(r + 1)
            return carry

        lax.fori_loop(0, R, step, 0)
        E1[u] = E0[...]
        for d in range(1, U):
            peer = lax.rem(u + d, U)
            rdma(E1.at[peer], E1.at[peer], s1.at[d], r1.at[peer], (t, pair)).wait_recv()
        whole = E1[0]
        for n in range(1, U):
            whole = whole + E1[n]
        E2[member] = whole

        def plane(act):
            n = 0
            for d in range(T):
                for half in (0, 1):
                    if d == 0 and half == 0:
                        continue
                    dev = (lax.rem(t + d, T), i if half == 0 else pair)
                    act(rdma(E2.at[member], E2.at[member], s2.at[n], r2.at[member], dev))
                    n += 1

        plane(lambda copy: copy.start())
        misfit_here(True)
        outs_here()
        outs_sent(SB.at[0, pl.ds(0, X)], 1)
        plane(lambda copy: copy.wait_send())
        for d in range(1, U):
            peer = lax.rem(u + d, U)
            rdma(E0, E1.at[u], s1.at[d], r1.at[u], (t, 2 * peer + h)).wait_send()
        for copy in pair_copies():
            copy.wait_send()

        def done(r, c):
            for side in (0, 1):
                @pl.when(side_here[side])
                def _():
                    edge_flow(r, side).wait_send()
            return c

        lax.fori_loop(0, R, done, 0)

    each_field(lambda copy: copy.wait_send())
    for d, peer in others_t:
        small_to(d, peer).wait_send()


def body(
    perm_field, step_multiplier, inflow, start_pressure, start_saturation,
    region_ids, region_table, well_cells, well_rates, observed,
):
    T = lax.axis_size("tm")
    N = lax.axis_size("space")
    X, Z, Y = start_pressure.shape
    W = well_cells.shape[0]
    members = perm_field.shape[0]
    assert members == T and T % 2 == 0 and N % 2 == 0 and X >= H and step_multiplier.shape[0] == 1
    well_row = (well_cells // Y).astype(jnp.float32)
    well_col = (well_cells % Y).astype(jnp.float32)
    small = jnp.concatenate(
        [well_rates, observed[:, 0, :], well_row[None], well_col[None]], axis=0
    ).T
    small = jnp.pad(small, ((0, 0), (0, 128 - small.shape[1])))
    R = T
    U = N // 2
    XU = 2 * X
    WL = XU + 2 * H
    f32 = jnp.float32
    cell = (Z, Y)
    block = (X, Z, Y)
    window = (WL, Z, Y)
    unit = (XU, Z, Y)

    def buf(*shape):
        return pltpu.VMEM(shape, f32)

    dma = pltpu.SemaphoreType.DMA
    vmem = pl.BlockSpec(memory_space=pltpu.VMEM)
    anyspace = pl.BlockSpec(memory_space=pl.ANY)
    out_shape = jax.ShapeDtypeStruct((1, members) + block, f32)
    mis, outp, outs = pl.pallas_call(
        functools.partial(kernel, T, N),
        out_shape=(jax.ShapeDtypeStruct((8, 128), f32), out_shape, out_shape),
        in_specs=[anyspace] * 6 + [pl.BlockSpec(memory_space=pltpu.SMEM)] + [vmem] * 2,
        out_specs=(vmem, anyspace, anyspace),
        scratch_shapes=[
            buf(2, *block), pltpu.VMEM(block, jnp.int32), buf(R, *block), buf(R, *window), buf(*window),
            buf(R, *window), buf(R, *block), buf(R + 1, *window), buf(R, 2, *cell), buf(T, W, 128),
            buf(2, *window), buf(2, *window), buf(2, *window), buf(2, *window), buf(*window),
            buf(*window), buf(ITERS, *window),
            pltpu.VMEM(unit, jnp.int32), buf(R + 1, *unit), buf(R + 1, *unit), buf(R, 2, *cell),
            buf(*unit), buf(*unit), buf(*unit), buf(W, 1), buf(8, 128), buf(U, 8, 128), buf(T, 8, 128),
            dma((5,)), dma((2, T // 2)), dma((2, T)), dma((2 * R + 2, 3)), dma((2 * R + 2, 3)),
            dma((R, 3)), dma((R, 3)), dma((R + 1, 2)), dma((R + 1, 2)), dma((T,)), dma((T,)),
            dma((2,)), dma((2,)), dma((R, 2)), dma((R, 2)),
            dma((R, 2)), dma((2, T)), dma(()), dma((max(U, 2),)), dma((U,)), dma((2 * T - 1,)), dma((T,)),
        ],
        compiler_params=pltpu.CompilerParams(
            has_side_effects=True, collective_id=0, vmem_limit_bytes=56 * 1024 * 1024
        ),
    )(
        perm_field, step_multiplier, inflow, start_pressure, start_saturation, region_ids,
        region_table, small, well_row[None],
    )
    return mis[0, :members], outp, outs


def solution(mesh):
    return jax.shard_map(
        body,
        mesh=mesh,
        in_specs=(
            P(None, "space", None, None),
            P("tm", "space", None, None),
            P("tm", "space", None, None),
            P("space", None, None),
            P("space", None, None),
            P("space", None, None),
            P(),
            P(),
            P("tm", None),
            P(None, "tm", None),
        ),
        out_specs=(P(), P("tm", None, "space", None, None), P("tm", None, "space", None, None)),
        check_vma=False,
    )
```

time: 72.5 us -> 63.8 us (0.88)
  Pallas kernels: 65.6 us -> 56.9 us
    pallas_call x1, Pallas kernels: 65.6 us -> 56.9 us  [body(): pl.pallas_call(functools.partial(kernel, T, N), out_shape=(jax.ShapeDtype...]
where the time goes in v1:
time: 63.8 us; the launch traced here: 63.6 us
  Pallas kernels  56.9 us (89%)
  local copies, waits for them, and re-layouts  5.95 us (9%)
  between operations  0.68 us (1%)
    pallas_call x1, Pallas kernels, body(): pl.pallas_call(functools.partial(kernel, T, N), out_shape=(jax.ShapeDtype...  56.9 us
    unnamed x12, local copies, waits for them, and re-layouts  4.06 us

profile of v1, /device:TPU:0, one launch (start us, length us, event | category | flops | bytes accessed | tf_op | source)
XLA Modules:
  0.0 63.6 jit_solution(16276458501895664003)
XLA Ops:
  0.6 0.0 copy-start.4
  0.6 0.6 %copy-done.4 = s32[32]{0:T(128)S(1)} copy-done((s32[32]{0:T(128)S(1)}, s32[32]{0:T(128)}, u32[]{:S(2)}) %copy-start.4) | copy-done | bytes 152
  1.3 0.0 copy-start.1
  1.3 0.0 copy-start.2
  1.3 0.0 copy-start.3
  1.3 0.5 copy-done.1
  1.8 0.2 copy-done.2
  2.0 0.0 copy-done.3
  2.0 0.1 copy.17
  2.1 0.6 pad.4.small
  2.7 56.9 %shard_map.121 = (f32[8,128]{1,0:T(8,128)}, f32[1,4,4,32,256]{4,3,2,1,0:T(8,128)}, f32[1,4,4,32,256]{4,3,2,1,0:T(8,128)}) custom-call(f32[4,4,32,256]{3,2,1,0:T(8,128)} %perm.1, f32[1,4,32,256]{3,2,1,0:T(8,128)} %mult.1, f32[1,4,32,256]{3,2,1,0:T(8,128)} %infl.1, f32[4,32,256]{2,1,0:T(8,128)} %p0.1, f32[4,32,256]{2,1,0:T(8,128)} %s0.1, s32[4,32,256]{2,1,0:T(8,128)} %ids.1, ...), custom_call_target="tpu_custom_call" | custom-call | tf_op jit(solution)/shard_map/pallas_call | solution.py:660
  59.6 1.2 %slice_bitcast_fusion = f32[4]{0:T(128)} fusion(f32[8,128]{1,0:T(8,128)} %get-tuple-element.6), kind=kLoop, calls=%fused_computation.8 | loop fusion | bytes 32 | tf_op jit(solution)/shard_map/squeeze | solution.py:684
  60.8 0.0 copy-start
  60.8 1.9 %copy.20 = f32[1,4,4,32,256]{4,3,2,1,0:T(8,128)} copy(f32[1,4,4,32,256]{4,3,2,1,0:T(8,128)} %get-tuple-element.15) | data formatting | bytes 1048576
  62.8 0.0 copy-done
  62.8 0.8 %copy.21 = f32[1,4,4,32,256]{4,3,2,1,0:T(8,128)} copy(f32[1,4,4,32,256]{4,3,2,1,0:T(8,128)S(1)} %copy-done) | data formatting | bytes 1048576
  (2 shorter events, 0.0 us)
Async XLA Ops:
  0.6 0.7 %copy-start.4 = (s32[32]{0:T(128)S(1)}, s32[32]{0:T(128)}, u32[]{:S(2)}) copy-start(s32[32]{0:T(128)} %param.17) | copy-start | bytes 388
  1.3 0.5 copy-start.1
  1.3 0.7 %copy-start.2 = (f32[4,1,32]{2,1,0:T(1,128)S(1)}, f32[4,1,32]{2,1,0:T(1,128)}, u32[]{:S(2)}) copy-start(f32[4,1,32]{2,1,0:T(1,128)} %param.19) | copy-start | bytes 1540
  1.3 0.7 %copy-start.3 = (f32[1,32]{1,0:T(1,128)S(1)}, f32[1,32]{1,0:T(1,128)}, u32[]{:S(2)}) copy-start(f32[1,32]{1,0:T(1,128)} %param.18) | copy-start | bytes 388
  60.8 1.9 %copy-start = (f32[1,4,4,32,256]{4,3,2,1,0:T(8,128)S(1)}, f32[1,4,4,32,256]{4,3,2,1,0:T(8,128)}, u32[]{:S(2)}) copy-start(f32[1,4,4,32,256]{4,3,2,1,0:T(8,128)} %get-tuple-element.16) | copy-start | bytes 1572868

commit v2 on v1

--- a/solution.py
+++ b/solution.py
@@ -23,17 +23,17 @@
 
 def kernel(
     T, N,
-    perm, mult, infl, p0, s0, ids, table, small, rows_row,
+    perm, mult, infl, p0, s0, ids, table, cells, rates, seen_in,
     mis, outp, outs,
     PM, IDS, MS, IW, CW, SA, SO, PB, PX, SM, RC, SS, EE, QI, BB, DD, WW,
     IDW, SB, FE, HF, V, G, Q, ES, E0, E1, E2,
-    lIN, sF, rF, sS, rS, sX, rX, sP, rP, sM, rM, sA, rA, sHF, rHF, sO, rO, lO, s1, r1, s2, r2,
+    lIN, sF, rF, sS, rS, sX, rX, sP, rP, sM, rM, sA, rA, sHF, rHF, sO, rO, lO, s1, r1, s2, r2, go,
 ):
     t = lax.axis_index("tm")
     i = lax.axis_index("space")
     X, Z, Y = IDS.shape
     R = T
-    W = small.shape[0]
+    W = cells.shape[1]
     U = N // 2
     XU = 2 * X
     WL = XU + 2 * H
@@ -45,9 +45,7 @@
     pair = i + 1 - 2 * h
     member = 2 * row + h
     own = H + h * X
-    toward = 2 * h - 1
     side_here = (u > 0, u < U - 1)
-    edge_there = jnp.logical_or(jnp.logical_and(h == 1, u < U - 1), jnp.logical_and(h == 0, u > 0))
 
     def load(n, src, dst):
         return pltpu.make_async_copy(src, dst, lIN.at[n])
@@ -110,27 +108,31 @@
             v = jnp.where(rock == k, table[which, k], v)
         return v
 
-    lane = lax.broadcasted_iota(jnp.int32, (W, small.shape[1]), 1)
-
-    def column(block, n):
-        return jnp.sum(jnp.where(lane == n, block, 0.0), axis=1, keepdims=True)
-
+    def upright(line):
+        eye = lax.broadcasted_iota(jnp.int32, (W, W), 0) == lax.broadcasted_iota(jnp.int32, (W, W), 1)
+        return jnp.sum(jnp.where(eye, line, 0.0), axis=1, keepdims=True)
+
+    bits = Y.bit_length() - 1
+    rows_row = jnp.right_shift(cells[...], bits).astype(jnp.float32)
+    cols_row = jnp.bitwise_and(cells[...], Y - 1).astype(jnp.float32)
     pick_cols = jnp.where(
-        lax.broadcasted_iota(jnp.int32, (W, Y), 1).astype(jnp.float32) == column(small[...], T + 2),
-        1.0, 0.0,
+        lax.broadcasted_iota(jnp.int32, (W, Y), 1).astype(jnp.float32) == upright(cols_row), 1.0, 0.0
     )
+    SM[t] = jnp.zeros(SM.shape[1:], jnp.float32)
+    SM[t, 0:1, 0:W] = rates[...]
+    SM[t, 1:1 + T, 0:W] = seen_in[...]
 
     def put_rows(first, count):
         base = (first * Z).astype(jnp.float32)
         return jnp.where(
-            lax.broadcasted_iota(jnp.int32, (count * Z, W), 0).astype(jnp.float32) == rows_row[...] - base,
+            lax.broadcasted_iota(jnp.int32, (count * Z, W), 0).astype(jnp.float32) == rows_row - base,
             1.0, 0.0,
         )
 
     others_t = [(d, lax.rem(t + d, T)) for d in range(1, T)]
 
     def small_to(d, peer):
-        return rdma(small, SM.at[t], sM.at[d], rM.at[t], (peer, i))
+        return rdma(SM.at[t], SM.at[t], sM.at[d], rM.at[t], (peer, i))
 
     def small_here(r):
         @pl.when(r != t)
@@ -138,7 +140,7 @@
             rdma(SM.at[r], SM.at[r], sM.at[1], rM.at[r], (r, i)).wait_recv()
 
     def source(r, rows, count):
-        rate = column(SM[r], 0)
+        rate = upright(SM[r, 0:1, 0:W])
         return jnp.dot(rows, pick_cols * rate, precision=EXACT).reshape(count, Z, Y)
 
     def field_to(rr):
@@ -211,66 +213,64 @@
             result = result + jnp.where(lanes == m, E2[m], 0.0)
         mis[...] = result * (1.0 / (R * W))
 
-    def spread(n, window, depth, same, other):
-        partner = rdma(
+    def edge_of(side, depth):
+        src = pl.ds(H + XU - depth if side else H, depth)
+        dst = pl.ds(H - depth if side else H + XU, depth)
+        return src, dst
+
+    def pooled(n, window, other):
+        return rdma(
             other.at[pl.ds(0, X)], window.at[pl.ds(own, X)], sS.at[n, 0], rS.at[n, 0], (t, pair)
         )
-        start = h * (X - depth)
-        there = pl.ds((1 - h) * (H + XU) + h * (H - depth), depth)
-        straight = rdma(
-            same.at[pl.ds(start, depth)], window.at[there], sS.at[n, 1], rS.at[n, 2 - h],
-            (t, i + 2 * toward),
-        )
-        aslant = rdma(
-            other.at[pl.ds(start, depth)], window.at[there], sS.at[n, 2], rS.at[n, 2 - h],
-            (t, i + toward),
-        )
-        return partner, straight, aslant
-
-    def spread_start(*args):
-        partner, straight, aslant = spread(*args)
-        partner.start()
-
-        @pl.when(edge_there)
-        def _():
-            straight.start()
-            aslant.start()
-
-    def spread_sent(*args):
-        partner, straight, aslant = spread(*args)
-        partner.wait_send()
-
-        @pl.when(edge_there)
-        def _():
-            straight.wait_send()
-            aslant.wait_send()
-
-    def spread_here(n, window, depth):
+
+    def halo(n, window, depth, side, relayed):
+        src, dst = edge_of(side, depth)
+        return rdma(
+            window.at[src], window.at[dst], sS.at[n, 1 + relayed], rS.at[n, 2 - side],
+            (t, i + 4 * side - 2),
+        )
+
+    def halos(n, window, depth, relayed, act):
+        for side in (0, 1):
+            @pl.when(jnp.logical_and(side_here[side], h == (1 - side if relayed else side)))
+            def _():
+                act(halo(n, window, depth, side, relayed))
+
+    def pool(n, window, depth, other):
+        pooled(n, window, other).start()
+        halos(n, window, depth, 0, lambda copy: copy.start())
+
+    def relay(n, window, depth, other):
         part = window.at[pl.ds(H + (1 - h) * X, X)]
         rdma(part, part, sS.at[n, 0], rS.at[n, 0], (t, pair)).wait_recv()
+        halos(n, window, depth, 1, lambda copy: copy.start())
+
+    def spread_here(n, window, depth, other):
         for side in (0, 1):
             @pl.when(side_here[side])
             def _():
                 part = window.at[pl.ds(H + XU if side else H - depth, depth)]
                 rdma(part, part, sS.at[n, 1], rS.at[n, 1 + side], (t, pair)).wait_recv()
 
+    def spread_sent(n, window, depth, other):
+        pooled(n, window, other).wait_send()
+        for relayed in (0, 1):
+            halos(n, window, depth, relayed, lambda copy: copy.wait_send())
+
     def own_of(window):
         return window.at[pl.ds(own, X)]
 
     def conduct_args(r):
-        return r, SA.at[r], H, own_of(SA.at[r]), SO.at[r]
+        return r, SA.at[r], H, SO.at[r]
 
     def inflow_args(r):
-        mine = own_of(IW.at[r])
-        return R + r, IW.at[r], H - 1, mine, mine
+        return R + r, IW.at[r], H - 1, own_of(IW.at[r])
 
     def pressure_args():
-        mine = own_of(PB.at[0])
-        return 2 * R, PB.at[0], H, mine, mine
+        return 2 * R, PB.at[0], H, own_of(PB.at[0])
 
     def storage_args():
-        mine = own_of(CW)
-        return 2 * R + 1, CW, H - 1, mine, mine
+        return 2 * R + 1, CW, H - 1, own_of(CW)
 
     def distribute(r):
         @pl.when(r != t)
@@ -280,13 +280,13 @@
         for x in range(X):
             SO[r, x] = jnp.sqrt(PM[1 - h, x] * MS[r, x])
             SA[r, own + x] = jnp.sqrt(PM[h, x] * MS[r, x])
-        spread_start(*conduct_args(r))
+        pool(*conduct_args(r))
 
         @pl.when(r != t)
         def _():
             mine = own_of(IW.at[r])
             rdma(mine, mine, sF.at[1, 0], rF.at[1, r], (r, i)).wait_recv()
-        spread_start(*inflow_args(r))
+        pool(*inflow_args(r))
 
     def round_of(k, side):
         if side == 0:
@@ -333,18 +333,24 @@
         infl_in.wait()
         perm_in.wait()
         meet()
-        spread_start(*pressure_args())
-        spread_start(*storage_args())
+        pool(*pressure_args())
+        pool(*storage_args())
         for d, peer in others_t:
             small_to(d, peer).start()
-        SM[t] = small[...]
         distribute(0)
+        pl.semaphore_signal(go, inc=1, device_id=(mate, i), device_id_type=MESH)
         send_fields()
         rows = put_rows(u * XU - H, WL)
+        local = upright(rows_row) - (u * (XU * Z)).astype(jnp.float32)
+        pick_rows = jnp.where(
+            lax.broadcasted_iota(jnp.int32, (W, XU * Z), 1).astype(jnp.float32) == local, 1.0, 0.0
+        )
+        owned = jnp.sum(pick_rows, axis=1, keepdims=True)
+        ES[...] = jnp.zeros(ES.shape, jnp.float32)
 
         def coefficients(r):
             slot = lax.rem(r, 2)
-            spread_here(r, SA.at[r], H)
+            spread_here(*conduct_args(r))
             handed(r)[0].start()
             for x in range(1, WL - 1):
                 a = SA[r, x]
@@ -355,14 +361,24 @@
                 EE[slot, x] = a * ss
             small_here(r)
             q = source(r, rows, WL)
-            spread_here(R + r, IW.at[r], H - 1)
+            spread_here(*inflow_args(r))
             for x in range(1, WL - 1):
                 QI[slot, x] = q[x] + IW[r, x]
 
-        spread_here(2 * R, PB.at[0], H)
-        spread_here(2 * R + 1, CW, H - 1)
+        def relay_fields(r):
+            relay(*conduct_args(r))
+            relay(*inflow_args(r))
+
+        relay(*pressure_args())
+        relay(*storage_args())
+        relay_fields(0)
+        distribute(1)
+        spread_here(*pressure_args())
+        spread_here(*storage_args())
         coefficients(0)
-        distribute(1)
+        relay_fields(1)
+        if R > 2:
+            distribute(2)
 
         def step(r, carry):
             slot = lax.rem(r, 2)
@@ -420,112 +436,11 @@
             PX[r, 0] = last(H - 1)
             PX[r, 1] = last(H + XU)
             handed(r)[2].start()
-
-            @pl.when(r < R - 1)
-            def _():
-                coefficients(r + 1)
-
-            @pl.when(r < R - 2)
-            def _():
-                distribute(r + 2)
-            return carry
-
-        lax.fori_loop(0, R, step, 0)
-        misfit_here(False)
-        outs_here()
-        outs_sent(PB.at[0, pl.ds(0, X)], 0)
-
-        def done(r, c):
-            spread_sent(*conduct_args(r))
-            spread_sent(*inflow_args(r))
-            for copy in handed(r):
-                copy.wait_send()
-
-            @pl.when(r > 0)
-            def _():
-                for side in (0, 1):
-                    @pl.when(side_here[side])
-                    def _():
-                        round_of(r, side).wait_send()
-            return c
-
-        lax.fori_loop(0, R, done, 0)
-        spread_sent(*pressure_args())
-        spread_sent(*storage_args())
-
-    @pl.when(core == 0)
-    def _():
-        def fraction(s, v):
-            sq = s * s
-            rest = (1.0 - s) * (1.0 - s)
-            return sq / (sq + v * rest)
-
-        def edge_flow(r, side):
-            src = FE.at[r, XU - 1 if side else 0]
-            return rdma(
-                src, HF.at[r, 1 - side], sHF.at[r, side], rHF.at[r, 1 - side], (t, i + 4 * side - 2)
-            )
-
-        def send_flow(r):
-            for side in (0, 1):
-                @pl.when(side_here[side])
-                def _():
-                    edge_flow(r, side).start()
-
-        def pair_copies():
-            part = pl.ds(h * X, X)
-            return (
-                rdma(SB.at[0, part], SB.at[0, part], sA.at[0], rA.at[0], (t, pair)),
-                rdma(IDW.at[part], IDW.at[part], sA.at[1], rA.at[1], (t, pair)),
-            )
-
-        for side in (0, 1):
-            @pl.when(jnp.logical_not(side_here[side]))
-            def _():
-                def clear(r, c):
-                    HF[r, side] = zero
-                    return c
-
-                lax.fori_loop(0, R, clear, 0)
-
-        mult_in.wait()
-        infl_in.wait()
-        s0_in.wait()
-        ids_win.wait()
-        meet()
-        send_fields()
-        for d, peer in others_t:
-            small_to(d, peer).start()
-        SM[t] = small[...]
-        for copy in pair_copies():
-            copy.start()
-        rows = put_rows(u * XU, XU)
-        local = column(small[...], T + 1) - (u * (XU * Z)).astype(jnp.float32)
-        pick_rows = jnp.where(
-            lax.broadcasted_iota(jnp.int32, (W, XU * Z), 1).astype(jnp.float32) == local, 1.0, 0.0
-        )
-        owned = jnp.sum(pick_rows, axis=1, keepdims=True)
-        there = pl.ds((1 - h) * X, X)
-        rdma(SB.at[0, there], SB.at[0, there], sA.at[0], rA.at[0], (t, pair)).wait_recv()
-        rdma(IDW.at[there], IDW.at[there], sA.at[1], rA.at[1], (t, pair)).wait_recv()
-        for x in range(XU):
-            rock = IDW[x]
-            V[x] = looked_up(rock, 1)
-            G[x] = 0.1 * looked_up(rock, 2)
-            FE[0, x] = fraction(SB[0, x], V[x])
-        send_flow(0)
-        ES[...] = jnp.zeros(ES.shape, jnp.float32)
-
-        def step(r, carry):
-            small_here(r)
-            q_all = source(r, rows, XU)
-            for x in range(XU):
-                Q[x] = q_all[x]
-            for copy in handed(r):
-                copy.wait_recv()
             seen = jnp.dot(pick_rows, PB[r + 1, H:H + XU].reshape(XU * Z, Y), precision=EXACT)
             predicted = jnp.sum(seen * pick_cols, axis=1, keepdims=True)
-            gap = predicted - column(SM[r], 1 + member)
+            lines = lax.broadcasted_iota(jnp.int32, SM.shape[1:], 0)
+            seen_row = jnp.sum(jnp.where(lines == 1 + member, SM[r], 0.0), axis=0, keepdims=True)
+            gap = predicted - upright(seen_row[:, :W])
             ES[...] = ES[...] + owned * gap * gap
 
             @pl.when(r == R - 1)
@@ -535,48 +450,17 @@
                     peer = lax.rem(u + d, U)
                     rdma(E0, E1.at[u], s1.at[d], r1.at[u], (t, 2 * peer + h)).start()
 
-            for side in (0, 1):
-                @pl.when(side_here[side])
-                def _():
-                    part = HF.at[r, side]
-                    rdma(part, part, sHF.at[r, side], rHF.at[r, side], (t, pair)).wait_recv()
-
-            def p_of(x):
-                return PX[r, 0] if x < 0 else (PX[r, 1] if x >= XU else PB[r + 1, H + x])
-
-            def f_of(x):
-                return HF[r, 0] if x < 0 else (HF[r, 1] if x >= XU else FE[r, x])
-
-            def face(ai, aj, pi, pj, fi, fj):
-                fall = pi - pj
-                return ai * aj * fall * jnp.where(fall > 0, fi, fj)
-
-            def across(x):
-                return face(SA[r, H + x - 1], SA[r, H + x], p_of(x - 1), p_of(x), f_of(x - 1), f_of(x))
-
-            low = across(0)
-            for x in range(XU):
-                high = across(x + 1)
-                a = SA[r, H + x]
-                p = p_of(x)
-                f = f_of(x)
-                s = SB[r, x]
-                q = Q[x]
-                cz = jnp.where(zi < Z - 1, face(a, after(a, 0), p, after(p, 0), f, after(f, 0)), 0.0)
-                cy = jnp.where(yi < Y - 1, face(a, after(a, 1), p, after(p, 1), f, after(f, 1)), 0.0)
-                out = (high - low) + (cz - before(cz, 0)) + (cy - before(cy, 1))
-                low = high
-                gained = jnp.maximum(q, 0.0) * (1.0 - s) - jnp.maximum(-q, 0.0) * f - out
-                s = s + G[x] * gained
-                SB[r + 1, x] = s
-                FE[r + 1, x] = fraction(s, V[x])
-                if x == X - 1:
-                    put_out(r, 0, SB.at[r + 1, pl.ds(0, X)], 1)
-            put_out(r, 1, SB.at[r + 1, pl.ds(X, X)], 1)
-
             @pl.when(r < R - 1)
             def _():
-                send_flow(r + 1)
+                coefficients(r + 1)
+
+            @pl.when(r < R - 2)
+            def _():
+                relay_fields(r + 2)
+
+            @pl.when(r < R - 3)
+            def _():
+                distribute(r + 3)
             return carry
 
         lax.fori_loop(0, R, step, 0)
@@ -602,13 +486,170 @@
         plane(lambda copy: copy.start())
         misfit_here(True)
         outs_here()
-        outs_sent(SB.at[0, pl.ds(0, X)], 1)
+        outs_sent(PB.at[0, pl.ds(0, X)], 0)
         plane(lambda copy: copy.wait_send())
         for d in range(1, U):
             peer = lax.rem(u + d, U)
             rdma(E0, E1.at[u], s1.at[d], r1.at[u], (t, 2 * peer + h)).wait_send()
+
+        def done(r, c):
+            spread_sent(*conduct_args(r))
+            spread_sent(*inflow_args(r))
+            for copy in handed(r):
+                copy.wait_send()
+
+            @pl.when(r > 0)
+            def _():
+                for side in (0, 1):
+                    @pl.when(side_here[side])
+                    def _():
+                        round_of(r, side).wait_send()
+            return c
+
+        lax.fori_loop(0, R, done, 0)
+        spread_sent(*pressure_args())
+        spread_sent(*storage_args())
+
+    @pl.when(core == 0)
+    def _():
+        def fraction(s, v):
+            sq = s * s
+            rest = (1.0 - s) * (1.0 - s)
+            return sq / (sq + v * rest)
+
+        def edge_flow(r, side):
+            src = FE.at[r, XU - 1 if side else 0]
+            return rdma(
+                src, HF.at[r, 1 - side], sHF.at[r, side], rHF.at[r, 1 - side], (t, i + 4 * side - 2)
+            )
+
+        def first_flow(act):
+            for side in (0, 1):
+                @pl.when(jnp.logical_and(side_here[side], h == side))
+                def _():
+                    src = FE.at[0, XU - 1 if side else 0]
+                    for n, hop in ((0, 2), (1, 1)):
+                        act(rdma(
+                            src, HF.at[0, 1 - side], sHF.at[0, n], rHF.at[0, 1 - side],
+                            (t, i + hop * (2 * side - 1)),
+                        ))
+
+        def prepare(start):
+            for x in range(X):
+                rock = IDW[start + x]
+                v = looked_up(rock, 1)
+                V[start + x] = v
+                G[start + x] = 0.1 * looked_up(rock, 2)
+                FE[0, start + x] = fraction(SB[0, start + x], v)
+
+        def pair_copies():
+            part = pl.ds(h * X, X)
+            return (
+                rdma(SB.at[0, part], SB.at[0, part], sA.at[0], rA.at[0], (t, pair)),
+                rdma(IDW.at[part], IDW.at[part], sA.at[1], rA.at[1], (t, pair)),
+            )
+
+        for side in (0, 1):
+            @pl.when(jnp.logical_not(side_here[side]))
+            def _():
+                def clear(r, c):
+                    HF[r, side] = zero
+                    return c
+
+                lax.fori_loop(0, R, clear, 0)
+
+        s0_in.wait()
+        ids_win.wait()
+        prepare(h * X)
+        mult_in.wait()
+        infl_in.wait()
+        meet()
+        send_fields()
+        first_flow(lambda copy: copy.start())
+        for d, peer in others_t:
+            small_to(d, peer).start()
+        rows = put_rows(u * XU, XU)
+        pl.semaphore_wait(go, 1)
+        for copy in pair_copies():
+            copy.start()
+        def sources(r):
+            small_here(r)
+            q_all = source(r, rows, XU)
+            for x in range(XU):
+                Q[x] = q_all[x]
+
+        sources(0)
+        there = pl.ds((1 - h) * X, X)
+        rdma(SB.at[0, there], SB.at[0, there], sA.at[0], rA.at[0], (t, pair)).wait_recv()
+        rdma(IDW.at[there], IDW.at[there], sA.at[1], rA.at[1], (t, pair)).wait_recv()
+        prepare((1 - h) * X)
+
+        def step(r, carry):
+            for copy in handed(r):
+                copy.wait_recv()
+            for side in (0, 1):
+                @pl.when(side_here[side])
+                def _():
+                    part = HF.at[r, side]
+                    rdma(part, part, sHF.at[r, side], rHF.at[r, side], (t, pair)).wait_recv()
+
+            def p_of(x):
+                return PX[r, 0] if x < 0 else (PX[r, 1] if x >= XU else PB[r + 1, H + x])
+
+            def f_of(x):
+                return HF[r, 0] if x < 0 else (HF[r, 1] if x >= XU else FE[r, x])
+
+            def face(ai, aj, pi, pj, fi, fj):
+                fall = pi - pj
+                return ai * aj * fall * jnp.where(fall > 0, fi, fj)
+
+            def across(x):
+                return face(SA[r, H + x - 1], SA[r, H + x], p_of(x - 1), p_of(x), f_of(x - 1), f_of(x))
+
+            def transport(x, low, high):
+                a = SA[r, H + x]
+                p = p_of(x)
+                f = f_of(x)
+                s = SB[r, x]
+                q = Q[x]
+                cz = jnp.where(zi < Z - 1, face(a, after(a, 0), p, after(p, 0), f, after(f, 0)), 0.0)
+                cy = jnp.where(yi < Y - 1, face(a, after(a, 1), p, after(p, 1), f, after(f, 1)), 0.0)
+                out = (high - low) + (cz - before(cz, 0)) + (cy - before(cy, 1))
+                gained = jnp.maximum(q, 0.0) * (1.0 - s) - jnp.maximum(-q, 0.0) * f - out
+                s = s + G[x] * gained
+                SB[r + 1, x] = s
+                FE[r + 1, x] = fraction(s, V[x])
+
+            for side in (0, 1):
+                x = XU - 1 if side else 0
+                transport(x, across(x), across(x + 1))
+
+                @pl.when(jnp.logical_and(r < R - 1, side_here[side]))
+                def _():
+                    edge_flow(r + 1, side).start()
+
+            low = across(1)
+            for x in range(1, XU - 1):
+                high = across(x + 1)
+                transport(x, low, high)
+                low = high
+                if x == X - 1:
+                    put_out(r, 0, SB.at[r + 1, pl.ds(0, X)], 1)
+            put_out(r, 1, SB.at[r + 1, pl.ds(X, X)], 1)
+
+            @pl.when(r < R - 1)
+            def _():
+                sources(r + 1)
+            return carry
+
+        lax.fori_loop(0, R, step, 0)
+        misfit_here(False)
+        outs_here()
+        outs_sent(SB.at[0, pl.ds(0, X)], 1)
         for copy in pair_copies():
             copy.wait_send()
+
+        first_flow(lambda copy: copy.wait_send())
 
         def done(r, c):
             for side in (0, 1):
@@ -617,11 +658,26 @@
                     edge_flow(r, side).wait_send()
             return c
 
-        lax.fori_loop(0, R, done, 0)
+        lax.fori_loop(1, R, done, 0)
 
     each_field(lambda copy: copy.wait_send())
     for d, peer in others_t:
         small_to(d, peer).wait_send()
+
+
+def deliver(mis_in, p_in, s_in, mis_out, p_out, s_out, row, done):
+    members = p_in.shape[1]
+    copies = []
+    for n, (src, dst) in enumerate(((p_in, p_out), (s_in, s_out))):
+        for m in range(members):
+            copies.append(pltpu.make_async_copy(src.at[0, m], dst.at[0, m], done.at[n * members + m]))
+    for copy in copies:
+        copy.start()
+    row[...] = mis_in[0, :members]
+    last = pltpu.make_async_copy(row, mis_out, done.at[2 * members])
+    last.start()
+    for copy in copies + [last]:
+        copy.wait()
 
 
 def body(
@@ -634,12 +690,7 @@
     W = well_cells.shape[0]
     members = perm_field.shape[0]
     assert members == T and T % 2 == 0 and N % 2 == 0 and X >= H and step_multiplier.shape[0] == 1
-    well_row = (well_cells // Y).astype(jnp.float32)
-    well_col = (well_cells % Y).astype(jnp.float32)
-    small = jnp.concatenate(
-        [well_rates, observed[:, 0, :], well_row[None], well_col[None]], axis=0
-    ).T
-    small = jnp.pad(small, ((0, 0), (0, 128 - small.shape[1])))
+    assert Y & (Y - 1) == 0
     R = T
     U = N // 2
     XU = 2 * X
@@ -659,12 +710,12 @@
     out_shape = jax.ShapeDtypeStruct((1, members) + block, f32)
     mis, outp, outs = pl.pallas_call(
         functools.partial(kernel, T, N),
-        out_shape=(jax.ShapeDtypeStruct((8, 128), f32), out_shape, out_shape),
-        in_specs=[anyspace] * 6 + [pl.BlockSpec(memory_space=pltpu.SMEM)] + [vmem] * 2,
-        out_specs=(vmem, anyspace, anyspace),
+        out_shape=(pltpu.VMEM((8, 128), f32), pltpu.VMEM(out_shape.shape, f32), pltpu.VMEM(out_shape.shape, f32)),
+        in_specs=[anyspace] * 6 + [pl.BlockSpec(memory_space=pltpu.SMEM)] + [vmem] * 3,
+        out_specs=(vmem, vmem, vmem),
         scratch_shapes=[
             buf(2, *block), pltpu.VMEM(block, jnp.int32), buf(R, *block), buf(R, *window), buf(*window),
-            buf(R, *window), buf(R, *block), buf(R + 1, *window), buf(R, 2, *cell), buf(T, W, 128),
+            buf(R, *window), buf(R, *block), buf(R + 1, *window), buf(R, 2, *cell), buf(T, 8 * (T // 8 + 1), 128),
             buf(2, *window), buf(2, *window), buf(2, *window), buf(2, *window), buf(*window),
             buf(*window), buf(ITERS, *window),
             pltpu.VMEM(unit, jnp.int32), buf(R + 1, *unit), buf(R + 1, *unit), buf(R, 2, *cell),
@@ -673,15 +724,26 @@
             dma((R, 3)), dma((R, 3)), dma((R + 1, 2)), dma((R + 1, 2)), dma((T,)), dma((T,)),
             dma((2,)), dma((2,)), dma((R, 2)), dma((R, 2)),
             dma((R, 2)), dma((2, T)), dma(()), dma((max(U, 2),)), dma((U,)), dma((2 * T - 1,)), dma((T,)),
+            pltpu.SemaphoreType.REGULAR,
         ],
         compiler_params=pltpu.CompilerParams(
-            has_side_effects=True, collective_id=0, vmem_limit_bytes=56 * 1024 * 1024
+            has_side_effects=True, collective_id=0, vmem_limit_bytes=44 * 1024 * 1024
         ),
     )(
         perm_field, step_multiplier, inflow, start_pressure, start_saturation, region_ids,
-        region_table, small, well_row[None],
+        region_table, well_cells[None], well_rates, observed[:, 0, :],
     )
-    return mis[0, :members], outp, outs
+    return pl.pallas_call(
+        deliver,
+        out_shape=(jax.ShapeDtypeStruct((members,), f32), out_shape, out_shape),
+        in_specs=[vmem, vmem, vmem],
+        out_specs=(anyspace, anyspace, anyspace),
+        scratch_shapes=[buf(members), dma((2 * members + 1,))],
+    )(
+        pltpu.with_memory_space_constraint(mis, pltpu.VMEM),
+        pltpu.with_memory_space_constraint(outp, pltpu.VMEM),
+        pltpu.with_memory_space_constraint(outs, pltpu.VMEM),
+    )
 
 
 def solution(mesh):

time: 63.8 us -> 55.1 us (0.86)
  Pallas kernels: 56.9 us -> 47.2 us
  local copies, waits for them, and re-layouts: 5.95 us -> 6.9 us
    pallas_call x1 -> x2, Pallas kernels: 56.9 us -> 47.2 us  [the longest x1 46.2 us: body(): pl.pallas_call(functools.partial(kernel, T, N), out_shape=(pltpu.VMEM((8,...]
    unnamed x12 -> x20, local copies, waits for them, and re-layouts: 4.06 us -> 6.9 us
    squeeze x1 -> x0, local copies, waits for them, and re-layouts: 1.19 us -> none  [body(): return (mis[0, :members], outp, outs)]
where the time goes in v2:
time: 55.1 us; the launch traced here: 54.8 us
  Pallas kernels  47.2 us (86%)
  local copies, waits for them, and re-layouts  6.9 us (13%)
  between operations  0.67 us (1%)
    pallas_call x1, Pallas kernels, body(): pl.pallas_call(functools.partial(kernel, T, N), out_shape=(pltpu.VMEM((8,...  46.2 us
    unnamed x20, local copies, waits for them, and re-layouts  6.9 us

profile of v2, /device:TPU:0, one launch (start us, length us, event | category | flops | bytes accessed | tf_op | source)
XLA Modules:
  0.0 54.8 jit_solution(13474444759529138500)
XLA Ops:
  0.6 0.0 copy-start.6
  0.6 0.0 copy-start.8
  0.7 0.0 copy-start.9
  0.7 0.7 %copy-done.6 = f32[3,8]{1,0:T(4,128)S(1)} copy-done((f32[3,8]{1,0:T(4,128)S(1)}, f32[3,8]{1,0:T(4,128)}, u32[]{:S(2)}) %copy-start.6) | copy-done | bytes 120
  1.3 0.0 copy-done.8
  1.3 0.0 copy-done.9
  1.3 0.0 copy-start
  1.3 1.0 %copy-done = f32[4,4,32,256]{3,2,1,0:T(8,128)S(1)} copy-done((f32[4,4,32,256]{3,2,1,0:T(8,128)S(1)}, f32[4,4,32,256]{3,2,1,0:T(8,128)}, u32[]{:S(2)}) %copy-start) | copy-done | bytes 524312
  2.4 0.0 copy-start.1
  2.4 0.9 %copy-done.1 = f32[1,4,32,256]{3,2,1,0:T(8,128)S(1)} copy-done((f32[1,4,32,256]{3,2,1,0:T(8,128)S(1)}, f32[1,4,32,256]{3,2,1,0:T(8,128)}, u32[]{:S(2)}) %copy-start.1) | copy-done | bytes 131096
  3.3 0.0 copy-start.2
  3.3 0.9 %copy-done.2 = f32[1,4,32,256]{3,2,1,0:T(8,128)S(1)} copy-done((f32[1,4,32,256]{3,2,1,0:T(8,128)S(1)}, f32[1,4,32,256]{3,2,1,0:T(8,128)}, u32[]{:S(2)}) %copy-start.2) | copy-done | bytes 131096
  4.2 0.0 copy-start.3
  4.2 0.9 %copy-done.3 = f32[4,32,256]{2,1,0:T(8,128)S(1)} copy-done((f32[4,32,256]{2,1,0:T(8,128)S(1)}, f32[4,32,256]{2,1,0:T(8,128)}, u32[]{:S(2)}) %copy-start.3) | copy-done | bytes 131096
  5.1 0.0 copy-start.4
  5.1 0.9 %copy-done.4 = f32[4,32,256]{2,1,0:T(8,128)S(1)} copy-done((f32[4,32,256]{2,1,0:T(8,128)S(1)}, f32[4,32,256]{2,1,0:T(8,128)}, u32[]{:S(2)}) %copy-start.4) | copy-done | bytes 131096
  6.0 0.0 copy-start.5
  6.0 0.9 %copy-done.5 = s32[4,32,256]{2,1,0:T(8,128)S(1)} copy-done((s32[4,32,256]{2,1,0:T(8,128)S(1)}, s32[4,32,256]{2,1,0:T(8,128)}, u32[]{:S(2)}) %copy-start.5) | copy-done | bytes 131096
  6.9 0.0 copy-start.7
  6.9 0.7 %copy-done.7 = f32[4,1,32]{2,1,0:T(1,128)S(1)} copy-done((f32[4,1,32]{2,1,0:T(1,128)S(1)}, f32[4,1,32]{2,1,0:T(1,128)}, u32[]{:S(2)}) %copy-start.7) | copy-done | bytes 536
  7.6 46.2 %shard_map.121 = (f32[8,128]{1,0:T(8,128)S(1)}, f32[1,4,4,32,256]{4,3,2,1,0:T(8,128)S(1)}, f32[1,4,4,32,256]{4,3,2,1,0:T(8,128)S(1)}) custom-call(f32[4,4,32,256]{3,2,1,0:T(8,128)S(1)} %copy-done, f32[1,4,32,256]{3,2,1,0:T(8,128)S(1)} %copy-done.1, f32[1,4,32,256]{3,2,1,0:T(8,128)S(1)} %copy-done.2, f32[4,32,256]{2,1,0:T(8,128)S(1)} %copy-done.3, ...), custom_call_target="tpu_custom_call" | custom-call | tf_op jit(solution)/shard_map/pallas_call | solution.py:711
  53.8 1.0 %shard_map.122 = (f32[4]{0:T(128)}, f32[1,4,4,32,256]{4,3,2,1,0:T(8,128)}, f32[1,4,4,32,256]{4,3,2,1,0:T(8,128)}) custom-call(f32[8,128]{1,0:T(8,128)S(1)} %get-tuple-element.6.mis_in, f32[1,4,4,32,256]{4,3,2,1,0:T(8,128)S(1)} %get-tuple-element.7.p_in, f32[1,4,4,32,256]{4,3,2,1,0:T(8,128)S(1)} %get-tuple-element.8.s_in), custom_call_target="tpu_custom_call" | custom-call | tf_op jit(solution)/shard_map/pallas_call | solution.py:736
Async XLA Ops:
  0.6 0.7 %copy-start.6 = (f32[3,8]{1,0:T(4,128)S(1)}, f32[3,8]{1,0:T(4,128)}, u32[]{:S(2)}) copy-start(f32[3,8]{1,0:T(4,128)} %table.1) | copy-start | bytes 292
  0.6 0.7 %copy-start.8 = (s32[32]{0:T(128)S(1)}, s32[32]{0:T(128)}, u32[]{:S(2)}) copy-start(s32[32]{0:T(128)} %param.17) | copy-start | bytes 388
  0.7 0.7 %copy-start.9 = (f32[1,32]{1,0:T(1,128)S(1)}, f32[1,32]{1,0:T(1,128)}, u32[]{:S(2)}) copy-start(f32[1,32]{1,0:T(1,128)} %rates.1) | copy-start | bytes 388
  1.3 1.0 %copy-start = (f32[4,4,32,256]{3,2,1,0:T(8,128)S(1)}, f32[4,4,32,256]{3,2,1,0:T(8,128)}, u32[]{:S(2)}) copy-start(f32[4,4,32,256]{3,2,1,0:T(8,128)} %perm.1) | copy-start | bytes 1572868
  2.4 0.9 %copy-start.1 = (f32[1,4,32,256]{3,2,1,0:T(8,128)S(1)}, f32[1,4,32,256]{3,2,1,0:T(8,128)}, u32[]{:S(2)}) copy-start(f32[1,4,32,256]{3,2,1,0:T(8,128)} %mult.1) | copy-start | bytes 393220
  3.3 0.9 %copy-start.2 = (f32[1,4,32,256]{3,2,1,0:T(8,128)S(1)}, f32[1,4,32,256]{3,2,1,0:T(8,128)}, u32[]{:S(2)}) copy-start(f32[1,4,32,256]{3,2,1,0:T(8,128)} %infl.1) | copy-start | bytes 393220
  4.2 0.9 %copy-start.3 = (f32[4,32,256]{2,1,0:T(8,128)S(1)}, f32[4,32,256]{2,1,0:T(8,128)}, u32[]{:S(2)}) copy-start(f32[4,32,256]{2,1,0:T(8,128)} %p0.1) | copy-start | bytes 393220
  5.1 0.9 %copy-start.4 = (f32[4,32,256]{2,1,0:T(8,128)S(1)}, f32[4,32,256]{2,1,0:T(8,128)}, u32[]{:S(2)}) copy-start(f32[4,32,256]{2,1,0:T(8,128)} %s0.1) | copy-start | bytes 393220
  6.0 0.9 %copy-start.5 = (s32[4,32,256]{2,1,0:T(8,128)S(1)}, s32[4,32,256]{2,1,0:T(8,128)}, u32[]{:S(2)}) copy-start(s32[4,32,256]{2,1,0:T(8,128)} %ids.1) | copy-start | bytes 393220
  6.9 0.7 %copy-start.7 = (f32[4,1,32]{2,1,0:T(1,128)S(1)}, f32[4,1,32]{2,1,0:T(1,128)}, u32[]{:S(2)}) copy-start(f32[4,1,32]{2,1,0:T(1,128)} %param.19) | copy-start | bytes 1540

commit v3 on v2

--- a/solution.py
+++ b/solution.py
@@ -373,12 +373,12 @@
         relay(*storage_args())
         relay_fields(0)
         distribute(1)
+        if R > 2:
+            distribute(2)
         spread_here(*pressure_args())
         spread_here(*storage_args())
         coefficients(0)
         relay_fields(1)
-        if R > 2:
-            distribute(2)
 
         def step(r, carry):
             slot = lax.rem(r, 2)
@@ -711,7 +711,7 @@
     mis, outp, outs = pl.pallas_call(
         functools.partial(kernel, T, N),
         out_shape=(pltpu.VMEM((8, 128), f32), pltpu.VMEM(out_shape.shape, f32), pltpu.VMEM(out_shape.shape, f32)),
-        in_specs=[anyspace] * 6 + [pl.BlockSpec(memory_space=pltpu.SMEM)] + [vmem] * 3,
+        in_specs=[pl.BlockSpec(memory_space=pltpu.HBM)] * 6 + [pl.BlockSpec(memory_space=pltpu.SMEM)] + [vmem] * 3,
         out_specs=(vmem, vmem, vmem),
         scratch_shapes=[
             buf(2, *block), pltpu.VMEM(block, jnp.int32), buf(R, *block), buf(R, *window), buf(*window),
@@ -727,7 +727,7 @@
             pltpu.SemaphoreType.REGULAR,
         ],
         compiler_params=pltpu.CompilerParams(
-            has_side_effects=True, collective_id=0, vmem_limit_bytes=44 * 1024 * 1024
+            has_side_effects=True, collective_id=0, vmem_limit_bytes=56 * 1024 * 1024
         ),
     )(
         perm_field, step_multiplier, inflow, start_pressure, start_saturation, region_ids,

time: 55.1 us -> 46.5 us (0.84)
  local copies, waits for them, and re-layouts: 6.9 us -> 0 us
  Pallas kernels: 47.2 us -> 45.7 us
    unnamed x20 -> x0, local copies, waits for them, and re-layouts: 6.9 us -> none
    pallas_call x1, Pallas kernels: 46.2 us -> 44.7 us  [body(): pl.pallas_call(functools.partial(kernel, T, N), out_shape=(pltpu.VMEM((8,...]
where the time goes in v3:
time: 46.5 us; the launch traced here: 46.3 us
  Pallas kernels  45.7 us (98%)
  between operations  0.64 us (1%)
    pallas_call x1, Pallas kernels, body(): pl.pallas_call(functools.partial(kernel, T, N), out_shape=(pltpu.VMEM((8,...  44.7 us
    pallas_call x1, Pallas kernels, body(): pl.pallas_call(deliver, out_shape=(jax.ShapeDtypeStruct((members,), f32),...  1.04 us

profile of v3, /device:TPU:0, one launch (start us, length us, event | category | flops | bytes accessed | tf_op | source)
XLA Modules:
  0.0 46.3 jit_solution(11504070886501800560)
XLA Ops:
  0.6 44.7 %shard_map.121 = (f32[8,128]{1,0:T(8,128)S(1)}, f32[1,4,4,32,256]{4,3,2,1,0:T(8,128)S(1)}, f32[1,4,4,32,256]{4,3,2,1,0:T(8,128)S(1)}) custom-call(f32[4,4,32,256]{3,2,1,0:T(8,128)} %perm.1, f32[1,4,32,256]{3,2,1,0:T(8,128)} %mult.1, f32[1,4,32,256]{3,2,1,0:T(8,128)} %infl.1, f32[4,32,256]{2,1,0:T(8,128)} %p0.1, f32[4,32,256]{2,1,0:T(8,128)} %s0.1, ...), custom_call_target="tpu_custom_call" | custom-call | tf_op jit(solution)/shard_map/pallas_call | solution.py:711
  45.3 1.0 %shard_map.122 = (f32[4]{0:T(128)}, f32[1,4,4,32,256]{4,3,2,1,0:T(8,128)}, f32[1,4,4,32,256]{4,3,2,1,0:T(8,128)}) custom-call(f32[8,128]{1,0:T(8,128)S(1)} %get-tuple-element.6.mis_in, f32[1,4,4,32,256]{4,3,2,1,0:T(8,128)S(1)} %get-tuple-element.7.p_in, f32[1,4,4,32,256]{4,3,2,1,0:T(8,128)S(1)} %get-tuple-element.8.s_in), custom_call_target="tpu_custom_call" | custom-call | tf_op jit(solution)/shard_map/pallas_call | solution.py:736

commit v4 on v3

--- a/solution.py
+++ b/solution.py
@@ -25,13 +25,13 @@
     T, N,
     perm, mult, infl, p0, s0, ids, table, cells, rates, seen_in,
     mis, outp, outs,
-    PM, IDS, MS, IW, CW, SA, SO, PB, PX, SM, RC, SS, EE, QI, BB, DD, WW,
+    PM, IR, MS, IW, CW, SA, SO, PB, PX, SM, RC, SS, EE, QI, BB, DD, WW,
     IDW, SB, FE, HF, V, G, Q, ES, E0, E1, E2,
     lIN, sF, rF, sS, rS, sX, rX, sP, rP, sM, rM, sA, rA, sHF, rHF, sO, rO, lO, s1, r1, s2, r2, go,
 ):
     t = lax.axis_index("tm")
     i = lax.axis_index("space")
-    X, Z, Y = IDS.shape
+    X, Z, Y = p0.shape
     R = T
     W = cells.shape[1]
     U = N // 2
@@ -57,7 +57,7 @@
 
     mult_in = load(0, mult.at[0], MS.at[t])
     infl_in = load(1, infl.at[0], IW.at[t, pl.ds(own, X)])
-    ids_in = load(2, ids, IDS)
+    ids_in = load(2, ids, IR.at[pl.ds(own, X)])
     perm_in = load(3, perm.at[pl.ds(2 * row, 2)], PM)
     p0_in = load(4, p0, PB.at[0, pl.ds(own, X)])
     s0_in = load(3, s0, SB.at[0, pl.ds(h * X, X)])
@@ -270,7 +270,7 @@
         return 2 * R, PB.at[0], H, own_of(PB.at[0])
 
     def storage_args():
-        return 2 * R + 1, CW, H - 1, own_of(CW)
+        return 2 * R + 1, IR, H - 1, own_of(IR)
 
     def distribute(r):
         @pl.when(r != t)
@@ -305,6 +305,11 @@
             rdma(PX.at[r], PX.at[r], sX.at[r, 2], rX.at[r, 2], dev),
         )
 
+    def ids_handed():
+        return rdma(
+            IR.at[pl.ds(H + (1 - h) * X, X)], IDW.at[pl.ds((1 - h) * X, X)], sA.at[1], rA.at[1], (mate, i)
+        )
+
     def meet():
         pl.semaphore_wait(barrier, (N - 1) + 2 * (T - 1))
 
@@ -312,7 +317,7 @@
     def _():
         ids_in.wait()
         for x in range(X):
-            CW[own + x] = looked_up(IDS[x], 0)
+            CW[own + x] = looked_up(IR[own + x], 0)
         for side in (0, 1):
             @pl.when(jnp.logical_not(side_here[side]))
             def _():
@@ -371,12 +376,21 @@
 
         relay(*pressure_args())
         relay(*storage_args())
+        ids_handed().start()
         relay_fields(0)
         distribute(1)
         if R > 2:
             distribute(2)
         spread_here(*pressure_args())
         spread_here(*storage_args())
+        for x in range(X):
+            CW[H + (1 - h) * X + x] = looked_up(IR[H + (1 - h) * X + x], 0)
+        for side in (0, 1):
+            @pl.when(side_here[side])
+            def _():
+                first = H + XU if side else 1
+                for x in range(first, first + H - 1):
+                    CW[x] = looked_up(IR[x], 0)
         coefficients(0)
         relay_fields(1)
 
@@ -509,6 +523,7 @@
         lax.fori_loop(0, R, done, 0)
         spread_sent(*pressure_args())
         spread_sent(*storage_args())
+        ids_handed().wait_send()
 
     @pl.when(core == 0)
     def _():
@@ -544,10 +559,7 @@
 
         def pair_copies():
             part = pl.ds(h * X, X)
-            return (
-                rdma(SB.at[0, part], SB.at[0, part], sA.at[0], rA.at[0], (t, pair)),
-                rdma(IDW.at[part], IDW.at[part], sA.at[1], rA.at[1], (t, pair)),
-            )
+            return (rdma(SB.at[0, part], SB.at[0, part], sA.at[0], rA.at[0], (t, pair)),)
 
         for side in (0, 1):
             @pl.when(jnp.logical_not(side_here[side]))
@@ -714,7 +726,7 @@
         in_specs=[pl.BlockSpec(memory_space=pltpu.HBM)] * 6 + [pl.BlockSpec(memory_space=pltpu.SMEM)] + [vmem] * 3,
         out_specs=(vmem, vmem, vmem),
         scratch_shapes=[
-            buf(2, *block), pltpu.VMEM(block, jnp.int32), buf(R, *block), buf(R, *window), buf(*window),
+            buf(2, *block), pltpu.VMEM(window, jnp.int32), buf(R, *block), buf(R, *window), buf(*window),
             buf(R, *window), buf(R, *block), buf(R + 1, *window), buf(R, 2, *cell), buf(T, 8 * (T // 8 + 1), 128),
             buf(2, *window), buf(2, *window), buf(2, *window), buf(2, *window), buf(*window),
             buf(*window), buf(ITERS, *window),

time: 46.5 us -> 45.8 us (0.985)
  Pallas kernels: 45.7 us -> 45 us
    pallas_call x1, Pallas kernels: 44.7 us -> 43.9 us  [body(): pl.pallas_call(functools.partial(kernel, T, N), out_shape=(pltpu.VMEM((8,...]
where the time goes in v4:
time: 45.8 us; the launch traced here: 45.6 us
  Pallas kernels  45 us (98%)
  between operations  0.64 us (1%)
    pallas_call x1, Pallas kernels, body(): pl.pallas_call(functools.partial(kernel, T, N), out_shape=(pltpu.VMEM((8,...  43.9 us
    pallas_call x1, Pallas kernels, body(): pl.pallas_call(deliver, out_shape=(jax.ShapeDtypeStruct((members,), f32),...  1.04 us

profile of v4, /device:TPU:0, one launch (start us, length us, event | category | flops | bytes accessed | tf_op | source)
XLA Modules:
  0.0 45.6 jit_solution(15341610633916582112)
XLA Ops:
  0.6 43.9 %shard_map.121 = (f32[8,128]{1,0:T(8,128)S(1)}, f32[1,4,4,32,256]{4,3,2,1,0:T(8,128)S(1)}, f32[1,4,4,32,256]{4,3,2,1,0:T(8,128)S(1)}) custom-call(f32[4,4,32,256]{3,2,1,0:T(8,128)} %perm.1, f32[1,4,32,256]{3,2,1,0:T(8,128)} %mult.1, f32[1,4,32,256]{3,2,1,0:T(8,128)} %infl.1, f32[4,32,256]{2,1,0:T(8,128)} %p0.1, f32[4,32,256]{2,1,0:T(8,128)} %s0.1, ...), custom_call_target="tpu_custom_call" | custom-call | tf_op jit(solution)/shard_map/pallas_call | solution.py:723
  44.6 1.0 %shard_map.122 = (f32[4]{0:T(128)}, f32[1,4,4,32,256]{4,3,2,1,0:T(8,128)}, f32[1,4,4,32,256]{4,3,2,1,0:T(8,128)}) custom-call(f32[8,128]{1,0:T(8,128)S(1)} %get-tuple-element.6.mis_in, f32[1,4,4,32,256]{4,3,2,1,0:T(8,128)S(1)} %get-tuple-element.7.p_in, f32[1,4,4,32,256]{4,3,2,1,0:T(8,128)S(1)} %get-tuple-element.8.s_in), custom_call_target="tpu_custom_call" | custom-call | tf_op jit(solution)/shard_map/pallas_call | solution.py:748

commit v5 on v4

--- a/solution.py
+++ b/solution.py
@@ -27,7 +27,7 @@
     mis, outp, outs,
     PM, IR, MS, IW, CW, SA, SO, PB, PX, SM, RC, SS, EE, QI, BB, DD, WW,
     IDW, SB, FE, HF, V, G, Q, ES, E0, E1, E2,
-    lIN, sF, rF, sS, rS, sX, rX, sP, rP, sM, rM, sA, rA, sHF, rHF, sO, rO, lO, s1, r1, s2, r2, go,
+    lIN, sF, rF, sS, rS, sX, rX, sP, rP, sM, rM, sA, rA, sHF, rHF, sO, rO, lO, s1, r1, s2, r2,
 ):
     t = lax.axis_index("tm")
     i = lax.axis_index("space")
@@ -343,7 +343,6 @@
         for d, peer in others_t:
             small_to(d, peer).start()
         distribute(0)
-        pl.semaphore_signal(go, inc=1, device_id=(mate, i), device_id_type=MESH)
         send_fields()
         rows = put_rows(u * XU - H, WL)
         local = upright(rows_row) - (u * (XU * Z)).astype(jnp.float32)
@@ -581,7 +580,6 @@
         for d, peer in others_t:
             small_to(d, peer).start()
         rows = put_rows(u * XU, XU)
-        pl.semaphore_wait(go, 1)
         for copy in pair_copies():
             copy.start()
         def sources(r):
@@ -736,7 +734,6 @@
             dma((R, 3)), dma((R, 3)), dma((R + 1, 2)), dma((R + 1, 2)), dma((T,)), dma((T,)),
             dma((2,)), dma((2,)), dma((R, 2)), dma((R, 2)),
             dma((R, 2)), dma((2, T)), dma(()), dma((max(U, 2),)), dma((U,)), dma((2 * T - 1,)), dma((T,)),
-            pltpu.SemaphoreType.REGULAR,
         ],
         compiler_params=pltpu.CompilerParams(
             has_side_effects=True, collective_id=0, vmem_limit_bytes=56 * 1024 * 1024

time: 45.8 us -> 45.1 us (0.985)
  Pallas kernels: 45 us -> 44.3 us
    pallas_call x1, Pallas kernels: 43.9 us -> 43.2 us  [body(): pl.pallas_call(functools.partial(kernel, T, N), out_shape=(pltpu.VMEM((8,...]
where the time goes in v5:
time: 45.1 us; the launch traced here: 44.9 us
  Pallas kernels  44.3 us (98%)
  between operations  0.64 us (1%)
    pallas_call x1, Pallas kernels, body(): pl.pallas_call(functools.partial(kernel, T, N), out_shape=(pltpu.VMEM((8,...  43.2 us
    pallas_call x1, Pallas kernels, body(): pl.pallas_call(deliver, out_shape=(jax.ShapeDtypeStruct((members,), f32),...  1.04 us

profile of v5, /device:TPU:0, one launch (start us, length us, event | category | flops | bytes accessed | tf_op | source)
XLA Modules:
  0.0 44.9 jit_solution(10234393032678701289)
XLA Ops:
  0.6 43.2 %shard_map.121 = (f32[8,128]{1,0:T(8,128)S(1)}, f32[1,4,4,32,256]{4,3,2,1,0:T(8,128)S(1)}, f32[1,4,4,32,256]{4,3,2,1,0:T(8,128)S(1)}) custom-call(f32[4,4,32,256]{3,2,1,0:T(8,128)} %perm.1, f32[1,4,32,256]{3,2,1,0:T(8,128)} %mult.1, f32[1,4,32,256]{3,2,1,0:T(8,128)} %infl.1, f32[4,32,256]{2,1,0:T(8,128)} %p0.1, f32[4,32,256]{2,1,0:T(8,128)} %s0.1, ...), custom_call_target="tpu_custom_call" | custom-call | tf_op jit(solution)/shard_map/pallas_call | solution.py:721
  43.9 1.0 %shard_map.122 = (f32[4]{0:T(128)}, f32[1,4,4,32,256]{4,3,2,1,0:T(8,128)}, f32[1,4,4,32,256]{4,3,2,1,0:T(8,128)}) custom-call(f32[8,128]{1,0:T(8,128)S(1)} %get-tuple-element.6.mis_in, f32[1,4,4,32,256]{4,3,2,1,0:T(8,128)S(1)} %get-tuple-element.7.p_in, f32[1,4,4,32,256]{4,3,2,1,0:T(8,128)S(1)} %get-tuple-element.8.s_in), custom_call_target="tpu_custom_call" | custom-call | tf_op jit(solution)/shard_map/pallas_call | solution.py:745
